TPU v7x, 64 devices: a 2x2x8 block of a 4x4x8 slice. The times are simulated.
64 devices in a mesh: rep: 8 (over x, y, core), dp: 8 (over z).
Axes of the slice: x: 2, y: 2, z: 8, core: 2. Of those that a mesh axis runs over, the one named last changes fastest.
The devices are a block of a 4x4x8 slice.
Arguments:
- x: bfloat16 [64, 4096, 512], P(('rep', 'dp')), parts along dimension 0
- dy: bfloat16 [64, 4096, 512], P(('rep', 'dp')), parts along dimension 0
- w_gate: bfloat16 [2, 512, 1280], P(None, 'dp')
- w_up: bfloat16 [2, 512, 1280], P(None, 'dp')
- w_down: bfloat16 [2, 1280, 512], P(None, 'dp')
- m_w_gate: float32 [2, 512, 1280], P(None, 'dp')
- m_w_up: float32 [2, 512, 1280], P(None, 'dp')
- m_w_down: float32 [2, 1280, 512], P(None, 'dp')
- v_w_gate: float32 [2, 512, 1280], P(None, 'dp')
- v_w_up: float32 [2, 512, 1280], P(None, 'dp')
- v_w_down: float32 [2, 1280, 512], P(None, 'dp')
Outputs:
- output 1: bfloat16 [16, 512, 1280], P('rep', 'dp'), parts along dimension 0
- output 2: bfloat16 [16, 512, 1280], P('rep', 'dp'), parts along dimension 0
- output 3: bfloat16 [16, 1280, 512], P('rep', 'dp'), parts along dimension 0
- output 4: float32 [16, 512, 1280], P('rep', 'dp'), parts along dimension 0
- output 5: float32 [16, 512, 1280], P('rep', 'dp'), parts along dimension 0
- output 6: float32 [16, 1280, 512], P('rep', 'dp'), parts along dimension 0
- output 7: float32 [16, 512, 1280], P('rep', 'dp'), parts along dimension 0
- output 8: float32 [16, 512, 1280], P('rep', 'dp'), parts along dimension 0
- output 9: float32 [16, 1280, 512], P('rep', 'dp'), parts along dimension 0
There are 8 independent parts. A program takes and returns all parts, laid end to end along the dimension named above; an argument that names none is the same for every part.
All inputs are finite; a program needn't handle non-finite values.
Results may differ from a plain program's by a relative error of at most 0.022.
Values are sent between devices in bfloat16 or wider.
A program may use at most 768 MiB of HBM per device.

v0:
```python
import jax
import jax.numpy as jnp
from jax import lax
from jax.sharding import PartitionSpec as P

NAMES = ("w_gate", "w_up", "w_down")


def matmul(a, w):
    return jnp.dot(a, w, preferred_element_type=jnp.float32).astype(jnp.bfloat16)


def normed(h):
    wide = h.astype(jnp.float32)
    scale = lax.rsqrt(jnp.mean(wide**2, -1, keepdims=True) + 1e-6)
    return (wide * scale).astype(jnp.bfloat16)


def layer(h, w):
    a = normed(h)
    gate = jnp.dot(a, w["w_gate"], preferred_element_type=jnp.float32)
    up = jnp.dot(a, w["w_up"], preferred_element_type=jnp.float32)
    return h + matmul((jax.nn.silu(gate) * up).astype(jnp.bfloat16), w["w_down"])


def adamw(w, m, v, g):
    m = 0.9 * m + 0.1 * g
    v = 0.95 * v + 0.05 * g * g
    step = m * lax.rsqrt(v + 1e-8) + 0.1 * w
    return (w - 0.02 * step).astype(jnp.bfloat16), m, v


def clipped(gradients, sum_of_squares, count):
    factor = jnp.minimum(1.0, 0.5 * lax.rsqrt(sum_of_squares / count + 1e-30))
    return [g * factor for g in gradients]


def solution(mesh):
    def fetched(weights, number):
        return {name: lax.all_gather(w[number], "dp", axis=0, tiled=True) for name, w in zip(NAMES, weights, strict=True)}

    def step(x, dy, *arrays):
        weights, m, v = (arrays[i : i + 3] for i in (0, 3, 6))
        layers = weights[0].shape[0]
        h, kept = x[0], []
        for number in range(layers):
            kept.append(h)
            h = layer(h, fetched(weights, number))
        by_h, mine = dy[0], [None] * layers
        for number in reversed(range(layers)):
            _, back = jax.vjp(lambda w, h: layer(h, w), fetched(weights, number), kept[number])
            by_w, by_h = back(by_h)
            mine[number] = [lax.psum_scatter(by_w[name], "dp", scatter_dimension=0, tiled=True) for name in NAMES]
        gradients = [jnp.stack([mine[number][i] for number in range(layers)]).astype(jnp.float32) for i in range(3)]
        squares = lax.psum(sum(jnp.sum(g * g) for g in gradients), "dp")
        gradients = clipped(gradients, squares, lax.psum(1, "dp") * sum(g.size for g in gradients))
        new = [adamw(w.astype(jnp.float32), m, v, g) for w, m, v, g in zip(weights, m, v, gradients, strict=True)]
        return tuple(one[which] for which in range(3) for one in new)

    states, cut = P(("rep", "dp"), None, None), P(None, "dp", None)
    return jax.shard_map(
        step,
        mesh=mesh,
        in_specs=(states, states) + (cut,) * 9,
        out_specs=(P("rep", "dp", None),) * 9,
        check_vma=False,
    )
```

profile of v0, /device:TPU:22, one launch (start us, length us, event | category | flops | bytes accessed | tf_op | source)
XLA Modules:
  0.0 545.2 jit_solution(13000543596491508222)
XLA Ops:
  14.8 6.4 %copy.20 = bf16[1,4096,512]{1,2,0:T(8,128)(2,1)} copy(bf16[1,4096,512]{2,1,0:T(8,128)(2,1)} %param.11) | data formatting | bytes 8388608 | tf_op args[0]
  21.2 3.1 fusion.15
  24.3 6.4 %copy.21 = bf16[1,4096,512]{1,2,0:T(8,128)(2,1)} copy(bf16[1,4096,512]{2,1,0:T(8,128)(2,1)} %param.12) | data formatting | bytes 8388608 | tf_op args[1]
  30.7 18.7 %all-gather.13.cloned.1.call-done = bf16[1,512,1280]{2,1,0:T(8,128)(2,1)} async-done(((bf16[1,64,1280]{2,1,0:T(8,128)(2,1)}), bf16[1,512,1280]{2,1,0:T(8,128)(2,1)}) %all-gather.13.cloned.1.call-update) | async-done | bytes 1310736 | tf_op jit(solution)/shard_map/all_gather | solution.py:40
  49.5 11.9 %fusion.47 = f32[4096,1280]{1,0:T(8,128)} fusion(bf16[1,4096,512]{1,2,0:T(8,128)(2,1)} %copy.20, f32[4096]{0:T(1024)S(1)} %add_rsqrt_fusion, bf16[1,512,1280]{2,1,0:T(8,128)(2,1)} %all-gather.13.cloned.1.call-done), kind=kOutput, calls=%fused_computation.57 | convolution fusion | flops 5375000576 | bytes 26492928 | tf_op jit(solution)/shard_map/dot_general | solution.py:21
  61.4 24.4 %all-gather.15.cloned.1.call-done = bf16[1,512,1280]{2,1,0:T(8,128)(2,1)} async-done(((bf16[1,64,1280]{2,1,0:T(8,128)(2,1)}), bf16[1,512,1280]{2,1,0:T(8,128)(2,1)}) %all-gather.15.cloned.1.call-update) | async-done | bytes 1310736 | tf_op jit(solution)/shard_map/all_gather | solution.py:40
  85.7 19.1 %multiply_convert_fusion.1 = (bf16[4096,1280]{1,0:T(8,128)(2,1)}, f32[4096,1280]{1,0:T(8,128)}) fusion(f32[4096,1280]{1,0:T(8,128)} %fusion.47, bf16[1,512,1280]{2,1,0:T(8,128)(2,1)} %all-gather.15.cloned.1.call-done, bf16[1,4096,512]{1,2,0:T(8,128)(2,1)} %copy.20, f32[4096]{0:T(1024)S(1)} %add_rsqrt_fusion), kind=kOutput, calls=%fused_computation.17 | convolution fusion | flops 5406457856 | bytes 57950208 | tf_op jit(solution)/shard_map/dot_general | solution.py:22
  104.9 17.1 %all-gather.17.cloned.1.call-done = bf16[1,1280,512]{2,1,0:T(8,128)(2,1)} async-done(((bf16[1,160,512]{2,1,0:T(8,128)(2,1)}), bf16[1,1280,512]{2,1,0:T(8,128)(2,1)}) %all-gather.17.cloned.1.call-update) | async-done | bytes 1310736 | tf_op jit(solution)/shard_map/all_gather | solution.py:40
  122.0 11.4 %fusion.19 = (f32[4096]{0:T(1024)S(1)}, bf16[4096,512]{0,1:T(8,128)(2,1)}) fusion(bf16[4096,1280]{1,0:T(8,128)(2,1)} %get-tuple-element.24, bf16[1,1280,512]{2,1,0:T(8,128)(2,1)} %all-gather.17.cloned.1.call-done, bf16[1,4096,512]{1,2,0:T(8,128)(2,1)} %copy.20), kind=kOutput, calls=%fused_computation.37 | convolution fusion | flops 5379190784 | bytes 20201472 | tf_op jit(solution)/shard_map/dot_general | solution.py:10
  134.0 24.1 %all-gather.21.cloned.1.call-done = bf16[1,1280,512]{2,1,0:T(8,128)(2,1)} async-done(((bf16[1,160,512]{2,1,0:T(8,128)(2,1)}), bf16[1,1280,512]{2,1,0:T(8,128)(2,1)}) %all-gather.21.cloned.1.call-update) | async-done | bytes 1310736 | tf_op jit(solution)/shard_map/all_gather | solution.py:40
  158.1 10.5 %convolution_convert_fusion.1 = bf16[4096,1280]{1,0:T(8,128)(2,1)} fusion(bf16[1,4096,512]{2,1,0:T(8,128)(2,1)} %param.12, bf16[1,1280,512]{2,1,0:T(8,128)(2,1)} %all-gather.21.cloned.1.call-done), kind=kOutput, calls=%fused_computation.21 | convolution fusion | flops 5373952000 | bytes 15990784 | tf_op jit(solution)/shard_map/transpose(jvp())/dot_general | solution.py:10
  168.7 25.6 %all-gather.23.cloned.1.call-done = bf16[1,512,1280]{2,1,0:T(8,128)(2,1)} async-done(((bf16[1,64,1280]{2,1,0:T(8,128)(2,1)}), bf16[1,512,1280]{2,1,0:T(8,128)(2,1)}) %all-gather.23.cloned.1.call-update) | async-done | bytes 1310736 | tf_op jit(solution)/shard_map/all_gather | solution.py:40
  194.2 11.9 %fusion.39 = f32[4096,1280]{1,0:T(8,128)} fusion(bf16[4096,512]{0,1:T(8,128)(2,1)} %get-tuple-element.27, f32[4096]{0:T(1024)S(1)} %fusion.79, bf16[1,512,1280]{2,1,0:T(8,128)(2,1)} %all-gather.23.cloned.1.call-done), kind=kOutput, calls=%fused_computation.54 | convolution fusion | flops 5375000576 | bytes 26492928 | tf_op jit(solution)/shard_map/jvp()/dot_general | solution.py:22
  206.1 24.2 %all-gather.19.cloned.1.call-done = bf16[1,512,1280]{2,1,0:T(8,128)(2,1)} async-done(((bf16[1,64,1280]{2,1,0:T(8,128)(2,1)}), bf16[1,512,1280]{2,1,0:T(8,128)(2,1)}) %all-gather.19.cloned.1.call-update) | async-done | bytes 1310736 | tf_op jit(solution)/shard_map/all_gather | solution.py:40
  230.3 28.9 %fusion.2 = (bf16[4096,1280]{1,0:T(8,128)(2,1)}, f32[4096,1280]{1,0:T(8,128)}) fusion(f32[4096,1280]{1,0:T(8,128)} %fusion.39, bf16[4096,1280]{1,0:T(8,128)(2,1)} %convolution_convert_fusion.1, bf16[1,512,1280]{2,1,0:T(8,128)(2,1)} %all-gather.19.cloned.1.call-done, bf16[4096,512]{0,1:T(8,128)(2,1)} %get-tuple-element.27, f32[4096]{0:T(1024)S(1)} %fusion.79), kind=kOutput, calls=%fused_computation.8 | convolution fusion | flops 5437915136 | bytes 68435968 | tf_op jit(solution)/shard_map/jvp()/dot_general | solution.py:21
  259.2 9.6 %convolution_convert_fusion.4 = bf16[512,1280]{1,0:T(8,128)(2,1)} fusion(bf16[4096,1280]{1,0:T(8,128)(2,1)} %get-tuple-element.28, bf16[4096,512]{0,1:T(8,128)(2,1)S(1)} %copy-done.2, f32[4096]{0:T(1024)S(1)} %fusion.79), kind=kOutput, calls=%fused_computation.51 | convolution fusion | flops 5375000576 | bytes 16007168 | tf_op jit(solution)/shard_map/transpose(jvp())/dot_general | solution.py:21
  268.9 15.5 %fusion.22 = bf16[4096,512]{0,1:T(8,128)(2,1)} fusion(bf16[4096,1280]{1,0:T(8,128)(2,1)} %convolution_convert_fusion.1, bf16[1,512,1280]{2,1,0:T(8,128)(2,1)S(1)} %copy-done.16, f32[4096,1280]{1,0:T(8,128)} %get-tuple-element.29), kind=kOutput, calls=%fused_computation.41 | convolution fusion | flops 5402263552 | bytes 36962304 | tf_op jit(solution)/shard_map/transpose(jvp())/dot_general | solution.py:22
  284.5 11.1 %fusion.21 = (f32[4096]{0:T(1024)S(1)}, bf16[4096,512]{0,1:T(8,128)(2,1)S(1)}) fusion(bf16[4096,512]{0,1:T(8,128)(2,1)S(1)} %copy-done.3, bf16[4096,512]{0,1:T(8,128)(2,1)} %fusion.22, bf16[4096,1280]{1,0:T(8,128)(2,1)} %get-tuple-element.28, bf16[1,512,1280]{2,1,0:T(8,128)(2,1)S(1)} %copy-done.17), kind=kOutput, calls=%fused_computation.39 | convolution fusion | flops 5379190784 | bytes 24395776 | tf_op jit(solution)/shard_map/transpose(jvp())/dot_general | solution.py:21
  295.7 2.8 fusion.25
  298.5 8.4 %convolution_convert_fusion = bf16[4096,1280]{1,0:T(8,128)(2,1)} fusion(bf16[4096,512]{0,1:T(8,128)(2,1)S(1)} %fusion.25, bf16[1,1280,512]{2,1,0:T(8,128)(2,1)S(1)} %copy-done.15), kind=kOutput, calls=%fused_computation.20 | convolution fusion | flops 5373952000 | bytes 15990784 | tf_op jit(solution)/shard_map/transpose(jvp())/dot_general | solution.py:10
  306.9 20.6 %fusion.32 = bf16[512,1280]{1,0:T(8,128)(2,1)} fusion(f32[4096,1280]{1,0:T(8,128)} %fusion.47, f32[4096,1280]{1,0:T(8,128)} %get-tuple-element.25, bf16[4096,1280]{1,0:T(8,128)(2,1)} %convolution_convert_fusion, bf16[1,4096,512]{1,2,0:T(8,128)(2,1)S(1)} %copy-done, f32[4096]{0:T(1024)S(1)} %copy-done.14), kind=kOutput, calls=%fused_computation.49 | convolution fusion | flops 5433327616 | bytes 57950208 | tf_op jit(solution)/shard_map/transpose(jvp())/dot_general | solution.py:21
  327.7 16.4 %fusion.36 = bf16[512,1280]{1,0:T(8,128)(2,1)} fusion(bf16[4096,1280]{1,0:T(8,128)(2,1)} %convolution_convert_fusion.1, bf16[4096,512]{0,1:T(8,128)(2,1)} %get-tuple-element.27, f32[4096]{0:T(1024)S(1)} %fusion.79, f32[4096,1280]{1,0:T(8,128)} %get-tuple-element.29), kind=kOutput, calls=%fused_computation.52 | convolution fusion | flops 5407113216 | bytes 36978688 | tf_op jit(solution)/shard_map/transpose(jvp())/dot_general | solution.py:22
  344.2 16.4 %fusion.35 = bf16[512,1280]{1,0:T(8,128)(2,1)} fusion(bf16[4096,1280]{1,0:T(8,128)(2,1)} %convolution_convert_fusion, f32[4096,1280]{1,0:T(8,128)} %fusion.47, bf16[1,4096,512]{1,2,0:T(8,128)(2,1)} %copy.20, f32[4096]{0:T(1024)S(1)} %copy-done.14), kind=kOutput, calls=%fused_computation.50 | convolution fusion | flops 5407113216 | bytes 36978688 | tf_op jit(solution)/shard_map/transpose(jvp())/dot_general | solution.py:22
  360.7 18.4 %fusion.29 = bf16[1280,512]{1,0:T(8,128)(2,1)} fusion(bf16[1,4096,512]{2,1,0:T(8,128)(2,1)} %param.12, f32[4096,1280]{1,0:T(8,128)} %fusion.39, f32[4096,1280]{1,0:T(8,128)} %get-tuple-element.29), kind=kOutput, calls=%fused_computation.48 | convolution fusion | flops 5400821760 | bytes 47448064 | tf_op jit(solution)/shard_map/transpose(jvp())/dot_general | solution.py:10
  379.3 10.6 %convolution_convert_fusion.5 = bf16[1280,512]{1,0:T(8,128)(2,1)} fusion(bf16[4096,1280]{1,0:T(8,128)(2,1)} %get-tuple-element.24, bf16[4096,512]{0,1:T(8,128)(2,1)} %copy-done.4), kind=kOutput, calls=%fused_computation.53 | convolution fusion | flops 5369364480 | bytes 15990784 | tf_op jit(solution)/shard_map/transpose(jvp())/dot_general | solution.py:10
  391.8 8.5 %reduce-scatter.13.cloned.1.call-done = bf16[64,1280]{1,0:T(8,128)(2,1)} async-done(((bf16[512,1280]{1,0:T(8,128)(2,1)}), bf16[64,1280]{1,0:T(8,128)(2,1)}) %reduce-scatter.13.cloned.1.call-update) | async-done | bytes 163856 | tf_op jit(solution)/shard_map/reduce_scatter | solution.py:53
  400.3 37.3 %reduce-scatter.11.cloned.1.call-done = bf16[64,1280]{1,0:T(8,128)(2,1)} async-done(((bf16[512,1280]{1,0:T(8,128)(2,1)}), bf16[64,1280]{1,0:T(8,128)(2,1)}) %reduce-scatter.11.cloned.1.call-update) | async-done | bytes 163856 | tf_op jit(solution)/shard_map/reduce_scatter | solution.py:53
  440.6 34.4 %reduce-scatter.17.cloned.1.call-done = bf16[160,512]{1,0:T(8,128)(2,1)} async-done(((bf16[1280,512]{1,0:T(8,128)(2,1)}), bf16[160,512]{1,0:T(8,128)(2,1)}) %reduce-scatter.17.cloned.1.call-update) | async-done | bytes 163856 | tf_op jit(solution)/shard_map/reduce_scatter | solution.py:53
  475.0 37.3 %reduce-scatter.15.cloned.1.call-done = bf16[160,512]{1,0:T(8,128)(2,1)} async-done(((bf16[1280,512]{1,0:T(8,128)(2,1)}), bf16[160,512]{1,0:T(8,128)(2,1)}) %reduce-scatter.15.cloned.1.call-update) | async-done | bytes 163856 | tf_op jit(solution)/shard_map/reduce_scatter | solution.py:53
  514.8 16.2 %psum.7 = f32[]{:T(128)} all-reduce(f32[]{:T(128)S(6)} %add.99), channel_id=1, replica_groups=mesh['rep'=8,'dp'=8] {'dp'}, use_global_device_ids=true, to_apply=%region_12.13 | all-reduce | flops 1 | bytes 8 | tf_op jit(solution)/shard_map/psum | solution.py:55
  531.6 2.8 fusion.75
  534.5 3.5 fusion.66
  (71 shorter events, 14.2 us)
Async XLA Ops:
  7.2 42.3 %all-gather.13.cloned.1.call-start = ((), (), s32[]{:S(2)}) async-start(), calls=%async_computation.12 | async-start | bytes 1474560 | tf_op jit(solution)/shard_map/all_gather | solution.py:40
  9.1 76.7 %all-gather.15.cloned.1.call-start = ((), (), s32[]{:S(2)}) async-start(), calls=%async_computation.13 | async-start | bytes 1474560 | tf_op jit(solution)/shard_map/all_gather | solution.py:40
  10.9 111.1 %all-gather.17.cloned.1.call-start = ((), (), s32[]{:S(2)}) async-start(), calls=%async_computation.14 | async-start | bytes 1474560 | tf_op jit(solution)/shard_map/all_gather | solution.py:40
  12.8 145.3 %all-gather.21.cloned.1.call-start = ((), (), s32[]{:S(2)}) async-start(), calls=%async_computation.16 | async-start | bytes 1474560 | tf_op jit(solution)/shard_map/all_gather | solution.py:40
  13.4 180.8 %all-gather.23.cloned.1.call-start = ((), (), s32[]{:S(2)}) async-start(), calls=%async_computation.17 | async-start | bytes 1474560 | tf_op jit(solution)/shard_map/all_gather | solution.py:40
  14.1 216.2 %all-gather.19.cloned.1.call-start = ((), (), s32[]{:S(2)}) async-start(), calls=%async_computation.15 | async-start | bytes 1474560 | tf_op jit(solution)/shard_map/all_gather | solution.py:40
  14.7 375.2 %reduce-scatter.9.cloned.1.call-start = ((), (), s32[]{:S(2)}) async-start(), calls=%async_computation.7 | async-start | bytes 1474560 | tf_op jit(solution)/shard_map/reduce_scatter | solution.py:53
  24.3 61.4 %copy-start.13 = (f32[4096]{0:T(1024)}, f32[4096]{0:T(1024)S(1)}, u32[]{:S(2)}) copy-start(f32[4096]{0:T(1024)S(1)} %add_rsqrt_fusion) | copy-start | bytes 49156
  133.4 0.6 copy-start.11
  230.3 28.9 %copy-start.2 = (bf16[4096,512]{0,1:T(8,128)(2,1)S(1)}, bf16[4096,512]{0,1:T(8,128)(2,1)}, u32[]{:S(2)}) copy-start(bf16[4096,512]{0,1:T(8,128)(2,1)} %get-tuple-element.27) | copy-start | bytes 12582916
  259.2 9.7 %copy-start.16 = (bf16[1,512,1280]{2,1,0:T(8,128)(2,1)S(1)}, bf16[1,512,1280]{2,1,0:T(8,128)(2,1)}, u32[]{:S(2)}) copy-start(bf16[1,512,1280]{2,1,0:T(8,128)(2,1)} %all-gather.23.cloned.1.call-done) | copy-start | bytes 3932164
  268.8 121.2 %reduce-scatter.7.cloned.1.call-start = ((), (), s32[]{:S(2)}) async-start(), calls=%async_computation.6 | async-start | bytes 1474560 | tf_op jit(solution)/shard_map/reduce_scatter | solution.py:53
  268.9 15.5 %copy-start.3 = (bf16[4096,512]{0,1:T(8,128)(2,1)S(1)}, bf16[4096,512]{0,1:T(8,128)(2,1)}, u32[]{:S(2)}) copy-start(bf16[4096,512]{0,1:T(8,128)(2,1)} %get-tuple-element.27) | copy-start | bytes 12582916
  268.9 15.5 %copy-start.17 = (bf16[1,512,1280]{2,1,0:T(8,128)(2,1)S(1)}, bf16[1,512,1280]{2,1,0:T(8,128)(2,1)}, u32[]{:S(2)}) copy-start(bf16[1,512,1280]{2,1,0:T(8,128)(2,1)} %all-gather.19.cloned.1.call-done) | copy-start | bytes 3932164
  284.4 11.2 %copy-start.12 = (f32[4096]{0:T(1024)S(1)}, f32[4096]{0:T(1024)}, u32[]{:S(2)}) copy-start(f32[4096]{0:T(1024)} %copy-done.11) | copy-start | bytes 49156
  284.5 11.2 %copy-start.1 = (bf16[1,4096,512]{1,2,0:T(8,128)(2,1)S(1)}, bf16[1,4096,512]{1,2,0:T(8,128)(2,1)}, u32[]{:S(2)}) copy-start(bf16[1,4096,512]{1,2,0:T(8,128)(2,1)} %copy.21) | copy-start | bytes 12582916
  295.7 2.8 copy-start.15
  298.5 8.4 %copy-start.4 = (bf16[4096,512]{0,1:T(8,128)(2,1)}, bf16[4096,512]{0,1:T(8,128)(2,1)S(1)}, u32[]{:S(2)}) copy-start(bf16[4096,512]{0,1:T(8,128)(2,1)S(1)} %fusion.25) | copy-start | bytes 12582916
  298.5 8.4 %copy-start = (bf16[1,4096,512]{1,2,0:T(8,128)(2,1)S(1)}, bf16[1,4096,512]{1,2,0:T(8,128)(2,1)}, u32[]{:S(2)}) copy-start(bf16[1,4096,512]{1,2,0:T(8,128)(2,1)} %copy.20) | copy-start | bytes 12582916
  298.5 8.4 %copy-start.14 = (f32[4096]{0:T(1024)S(1)}, f32[4096]{0:T(1024)}, u32[]{:S(2)}) copy-start(f32[4096]{0:T(1024)} %copy-done.13) | copy-start | bytes 49156
  327.6 72.7 %reduce-scatter.13.cloned.1.call-start = ((), (), s32[]{:S(2)}) async-start(), calls=%async_computation.9 | async-start | bytes 1474560 | tf_op jit(solution)/shard_map/reduce_scatter | solution.py:53
  344.1 93.5 %reduce-scatter.11.cloned.1.call-start = ((), (), s32[]{:S(2)}) async-start(), calls=%async_computation.8 | async-start | bytes 1474560 | tf_op jit(solution)/shard_map/reduce_scatter | solution.py:53
  360.6 114.4 %reduce-scatter.17.cloned.1.call-start = ((), (), s32[]{:S(2)}) async-start(), calls=%async_computation.11 | async-start | bytes 1474560 | tf_op jit(solution)/shard_map/reduce_scatter | solution.py:53
  379.1 152.5 %copy-start.7 = (bf16[2,160,512]{2,1,0:T(8,128)(2,1)S(1)}, bf16[2,160,512]{2,1,0:T(8,128)(2,1)}, u32[]{:S(2)}) copy-start(bf16[2,160,512]{2,1,0:T(8,128)(2,1)} %param.15) | copy-start | bytes 983044
  379.2 155.3 %copy-start.5 = (bf16[2,64,1280]{2,1,0:T(8,128)(2,1)S(1)}, bf16[2,64,1280]{2,1,0:T(8,128)(2,1)}, u32[]{:S(2)}) copy-start(bf16[2,64,1280]{2,1,0:T(8,128)(2,1)} %param.13) | copy-start | bytes 983044
  379.2 155.3 %copy-start.6 = (bf16[2,64,1280]{2,1,0:T(8,128)(2,1)S(1)}, bf16[2,64,1280]{2,1,0:T(8,128)(2,1)}, u32[]{:S(2)}) copy-start(bf16[2,64,1280]{2,1,0:T(8,128)(2,1)} %param.14) | copy-start | bytes 983044
  379.2 155.3 %copy-start.8 = (f32[2,64,1280]{2,1,0:T(8,128)S(1)}, f32[2,64,1280]{2,1,0:T(8,128)}, u32[]{:S(2)}) copy-start(f32[2,64,1280]{2,1,0:T(8,128)} %param.19) | copy-start | bytes 1966084
  379.2 155.2 %copy-start.9 = (f32[2,64,1280]{2,1,0:T(8,128)S(1)}, f32[2,64,1280]{2,1,0:T(8,128)}, u32[]{:S(2)}) copy-start(f32[2,64,1280]{2,1,0:T(8,128)} %param.16) | copy-start | bytes 1966084
  379.2 155.2 %copy-start.10 = (f32[2,64,1280]{2,1,0:T(8,128)S(1)}, f32[2,64,1280]{2,1,0:T(8,128)}, u32[]{:S(2)}) copy-start(f32[2,64,1280]{2,1,0:T(8,128)} %param.20) | copy-start | bytes 1966084
  379.2 133.1 %reduce-scatter.15.cloned.1.call-start = ((), (), s32[]{:S(2)}) async-start(), calls=%async_computation.10 | async-start | bytes 1474560 | tf_op jit(solution)/shard_map/reduce_scatter | solution.py:53
Sparse Core Ops, SparseCore 0:
  10.2 39.2 all-gather.12
  51.6 34.0 all-gather.14
  87.9 34.0 all-gather.16
  124.0 34.0 all-gather.20
  160.1 34.0 all-gather.22
  196.2 34.0 all-gather.18
  269.0 34.9 reduce-scatter.8
  327.7 35.0 reduce-scatter.6
  365.1 35.0 reduce-scatter.12
  402.5 35.0 reduce-scatter.10
  439.9 35.0 reduce-scatter.16
  477.2 35.0 reduce-scatter.14
where the time goes:
time: 555 us; the launch traced here: 545 us
  waiting for transfers between devices  254 us (46%)
  matrix products  221 us (40%)
  local copies, waits for them, and re-layouts  18.7 us (3%)
  between operations  17.6 us (3%)
  other arithmetic  17.5 us (3%)
  blocking collectives  16.2 us (3%)
    all_gather x6, waiting for transfers between devices, fetched(): lax.all_gather(w[number], 'dp', axis=0, tiled=True)  134 us
    reduce_scatter x6, waiting for transfers between devices, step(): lax.psum_scatter(by_w[name], 'dp', scatter_dimension=0, tiled=True)  118 us
    dot_general x5, matrix products, layer(): gate = jnp.dot(a, w['w_gate'], preferred_element_type=jnp.float32)  82.1 us
    dot_general x5, matrix products, layer(): up = jnp.dot(a, w['w_up'], preferred_element_type=jnp.float32)  79.2 us
    dot_general x5, matrix products, matmul(): jnp.dot(a, w, preferred_element_type=jnp.float32).astype(jnp.bfloat16)  59.3 us
    psum x1, blocking collectives, step(): squares = lax.psum(sum((jnp.sum(g * g) for g in gradients)), 'dp')  16.2 us
    unnamed x38, local copies, waits for them, and re-layouts  13.5 us
  transfers between devices with their start and end apart: 12, of which 10 were waited for; matrix products, arithmetic and copies ran while one was open for 38% of the time, Pallas kernels for 0%

commit v1 on v0

v1 whole, which is shorter than its diff:
```python
import functools

import jax
import jax.numpy as jnp
from jax import lax
from jax.experimental import pallas as pl
from jax.experimental.pallas import tpu as pltpu
from jax.sharding import PartitionSpec as P

BF, F32 = jnp.bfloat16, jnp.float32
C = 256
TILES = 4
A, B = 0, 1
RIGHT, LEFT = 0, 1


def dot(a, b, ca=1, cb=0):
    return lax.dot_general(a, b, (((ca,), (cb,)), ((), ())), preferred_element_type=F32)


def sigmoid(g):
    return 0.5 * jnp.tanh(0.5 * g) + 0.5


def normed(h):
    return (h * lax.rsqrt(jnp.mean(h * h, -1, keepdims=True) + 1e-6)).astype(BF)


def when(condition):
    return (lambda body: body()) if condition is True else pl.when(condition)


def routes(n):
    far, near = n // 2, n - 1 - n // 2
    hops = {(A, RIGHT): far, (A, LEFT): near, (B, RIGHT): near, (B, LEFT): far}
    number, k = {}, 0
    for (m, d), count in hops.items():
        for hop in range(1, count + 1):
            number[m, d, hop] = k
            k += 1
    return hops, number, k


def step_kernel(
    n, layers, d_model, ff, tokens,
    x_hbm, dy_hbm, wg_hbm, wu_hbm, wd_hbm,
    gg_ref, gu_ref, gd_ref, squares_ref, a_hbm,
    x, a, dy, da, hidden, wgu, wd, dgu, hid, acc, dwd, buf, bufd, ss, ssd, others,
    local_sem, own_sem, ag_recv, ag_send, pair_recv, pair_send, rs_recv, rs_send, rsd_recv, rsd_send, sq_recv, sq_send, credit,
):
    me, rep = lax.axis_index("dp"), lax.axis_index("rep")
    core = lax.rem(rep, 2)
    partner = {"rep": rep + 1 - 2 * core}
    ring = lambda off: lax.rem(me + off + n, n)
    to = {RIGHT: {"dp": ring(1)}, LEFT: {"dp": ring(-1)}}
    sign = {RIGHT: 1, LEFT: -1}
    hops, number, messages = routes(n)
    far = n // 2
    chunks = ff // C
    rows_gu, rows_d = d_model // n, ff // n
    half_gu, half_d = rows_gu // 2, rows_d // 2
    half_w = d_model // 2
    tile = tokens // TILES
    MESH = pl.DeviceIdType.MESH

    barrier = pltpu.get_barrier_semaphore()
    for off in range(1, n):
        pl.semaphore_signal(barrier, inc=1, device_id={"dp": ring(off)}, device_id_type=MESH)
    pl.semaphore_signal(barrier, inc=1, device_id=partner, device_id_type=MESH)
    mine_gu = pl.ds(pl.multiple_of(me * rows_gu, rows_gu), rows_gu)
    mine_d = pl.ds(pl.multiple_of(me * rows_d, rows_d), rows_d)
    own = []
    for l in range(layers):
        for c in range(chunks):
            for m, src in ((0, wg_hbm), (1, wu_hbm)):
                own.append((src.at[l, :, pl.ds(c * C, C)], wgu.at[l, c, mine_gu, pl.ds(m * C, C)]))
        own.append((wd_hbm.at[l], wd.at[l, mine_d]))
    own = [pltpu.make_async_copy(s, t, own_sem.at[i]) for i, (s, t) in enumerate(own)]
    for copy in own:
        copy.start()
    load_x = pltpu.make_async_copy(x_hbm, x, local_sem.at[0])
    load_dy = pltpu.make_async_copy(dy_hbm, dy, local_sem.at[1])
    load_x.start()
    load_dy.start()
    pl.semaphore_wait(barrier, n)
    for copy in own:
        copy.wait()

    units = [(0, 0, 1), (0, 1, 2), (0, 3, chunks - 3), (0, None, None), (1, 0, 3), (1, 3, chunks - 3), (1, None, None)]

    def piece(u, m, owner):
        l, c, count = units[u]
        if c is None:
            return wd.at[l, pl.ds(pl.multiple_of(owner * rows_d + core * half_d, half_d), half_d), pl.ds(m * half_w, half_w)]
        return wgu.at[l, pl.ds(c, count), pl.ds(pl.multiple_of(owner * rows_gu + core * half_gu, half_gu), half_gu), pl.ds(m * C, C)]

    def everything(u):
        l, c, count = units[u]
        if c is None:
            return wd.at[l, pl.ds(0, messages * half_d), pl.ds(0, half_w)]
        return wgu.at[l, pl.ds(c, count), pl.ds(0, messages * half_gu), pl.ds(0, C)]

    def gather(u, k):
        for (m, d), count in hops.items():
            if k > count:
                continue
            block = piece(u, m, ring(-sign[d] * k))
            if k:
                pltpu.make_async_copy(block, block, ag_recv.at[u, number[m, d, k]]).wait()
            if k < count:
                pltpu.make_async_remote_copy(
                    src_ref=block, dst_ref=block, send_sem=ag_send.at[u], recv_sem=ag_recv.at[u, number[m, d, k + 1]],
                    device_id=to[d], device_id_type=MESH,
                ).start()
            if k:
                pltpu.make_async_remote_copy(
                    src_ref=block, dst_ref=block, send_sem=pair_send.at[u], recv_sem=pair_recv.at[u],
                    device_id=partner, device_id_type=MESH,
                ).start()

    def gathered(u):
        pltpu.make_async_copy(everything(u), everything(u), pair_recv.at[u]).wait()

    def rs_parts(down, s):
        if down:
            l = s
            return rows_d, half_w, dwd.at[l], bufd.at[l], rsd_recv, rsd_send.at[l], l
        slot = lax.rem(s, 2)
        return rows_gu, C, acc.at[slot], buf.at[slot], rs_recv, rs_send.at[slot], slot

    def rs_step(down, s, k, wait_credit=None):
        rows, width, total, slots, recv, send, slot = rs_parts(down, s)
        if k == 0 and wait_credit is not None:

            @when(wait_credit)
            def _():
                pl.semaphore_wait(credit.at[0], 1)
                pl.semaphore_wait(credit.at[1], 1)

        out = []
        for i, ((m, d), count) in enumerate(hops.items()):
            if k >= count:
                continue
            owner = ring(sign[d] * (count - k))
            term = total[pl.ds(pl.multiple_of(owner * rows, rows), rows), pl.ds(m * width, width)]
            if k == 0:
                at = messages + i
            else:
                at = number[m, d, k]
                pltpu.make_async_copy(slots.at[at], slots.at[at], recv.at[slot, at]).wait()
                term = term + slots[at].astype(F32)
            slots[at] = term.astype(BF)
            out.append((m, d, at))
        for m, d, at in out:
            there = number[m, d, k + 1]
            pltpu.make_async_remote_copy(
                src_ref=slots.at[at], dst_ref=slots.at[there], send_sem=send, recv_sem=recv.at[slot, there],
                device_id=to[d], device_id_type=MESH,
            ).start()

    def rs_final(down, s, l, c, give=None):
        rows, width, total, slots, recv, send, slot = rs_parts(down, s)
        sums = ssd if down else ss
        for m in (A, B):
            g = total[pl.ds(pl.multiple_of(me * rows, rows), rows), pl.ds(m * width, width)]
            for d in (RIGHT, LEFT):
                at = number[m, d, hops[m, d]]
                pltpu.make_async_copy(slots.at[at], slots.at[at], recv.at[slot, at]).wait()
                g = g + slots[at].astype(F32)
            g = g.astype(BF)
            if down:
                gd_ref[l, :, pl.ds(m * width, width)] = g
            else:
                (gg_ref, gu_ref)[m][l, :, pl.ds(pl.multiple_of(c * C, C), C)] = g
            wide = g.astype(F32)
            sums[...] += wide * wide
        pltpu.make_async_copy(slots.at[pl.ds(0, messages)], slots.at[pl.ds(0, messages)], send).wait()
        if give is not None:

            @when(give)
            def _():
                pl.semaphore_signal(credit.at[0], inc=1, device_id=to[LEFT], device_id_type=MESH)
                pl.semaphore_signal(credit.at[1], inc=1, device_id=to[RIGHT], device_id_type=MESH)

    def tile_rows(t):
        return pl.ds(pl.multiple_of(t * tile, tile), tile)

    gather(0, 0)
    gather(1, 0)
    ss[...] = jnp.zeros_like(ss)
    ssd[...] = jnp.zeros_like(ssd)
    load_x.wait()

    def first_norm(lo, hi):
        @pl.loop(lo, hi)
        def _(t):
            r = tile_rows(t)
            a[r] = normed(x[r].astype(F32))

    first_norm(0, 2)
    gather(0, 1)
    gather(1, 1)
    gather(2, 0)
    first_norm(2, 4)
    save_a = pltpu.make_async_copy(a, a_hbm, local_sem.at[2])
    save_a.start()
    gather(0, 2)
    gather(1, 2)
    gather(2, 1)
    da[...] = jnp.zeros_like(da)
    gather(0, 3)
    gather(1, 3)
    gather(2, 2)
    load_dy.wait()
    gather(0, 4)
    gathered(0)

    before = {
        1: [(1, 4), (2, 3), (3, 0)],
        2: [(3, 1), (4, 0)],
        3: [(2, 4), (3, 2), (4, 1), (5, 0)],
        4: [(3, 3), (4, 2), (5, 1), (6, 0)],
    }
    ready = {1: 1, 3: 2}
    for c in range(chunks):
        for event in before.get(c, ()):
            gather(*event)
        if c in ready:
            gathered(ready[c])

        @pl.loop(0, TILES)
        def _(t):
            r = tile_rows(t)
            both = dot(a[r], wgu[0, c])
            g, u = both[:, :C], both[:, C:]
            hidden[r, c * C : (c + 1) * C] = (g * sigmoid(g) * u).astype(BF)

    for event in ((3, 4), (4, 3), (5, 2), (6, 1)):
        gather(*event)
    gathered(3)
    save_a.wait()
    between = {0: [], 1: [(4, 4), (5, 3), (6, 2)], 2: [(5, 4), (6, 3)], 3: [(6, 4)]}
    for t in range(TILES):
        for event in between[t]:
            gather(*event)
        r = pl.ds(t * tile, tile)
        out = dot(hidden[r], wd[0]).astype(BF)
        h = (x[r].astype(F32) + out.astype(F32)).astype(BF)
        x[r] = h
        a[r] = normed(h.astype(F32))
    for u in (4, 5, 6):
        gathered(u)

    def first_half(l, c, t, back):
        r = tile_rows(t)
        both = dot(a[r], wgu[l, c])
        g, u = both[:, :C], both[:, C:]
        wdc = wd[l, pl.ds(pl.multiple_of(c * C, C), C)]
        dh = dot(back[r], wdc, 1, 1).astype(BF).astype(F32)
        s = sigmoid(g)
        silu = g * s
        slope = s + silu * (1.0 - s)
        both = jnp.concatenate([(dh * u * slope).astype(BF), (dh * silu).astype(BF)], axis=1)
        dgu[r] = both
        if l == layers - 1:
            hid[r] = (silu * u).astype(BF)
            da[r] += dot(both, wgu[l, c], 1, 1)

    last = layers - 1

    @pl.loop(0, chunks)
    def _(c):
        first_half_1 = functools.partial(first_half, last, c, back=dy)

        @pl.when(c >= 1)
        def _():
            rs_step(False, c - 1, 0, c >= 3)

        @pl.when(c >= 2)
        def _():
            rs_step(False, c - 2, 3)

        first_half_1(t=0)
        first_half_1(t=1)

        @pl.when(c >= 1)
        def _():
            rs_step(False, c - 1, 1)

        @pl.when(c >= 2)
        def _():
            rs_final(False, c - 2, last, c - 2, c >= 0)

        first_half_1(t=2)
        first_half_1(t=3)

        @pl.when(c >= 1)
        def _():
            rs_step(False, c - 1, 2)

        acc[lax.rem(c, 2)] = dot(a[...], dgu[...], 0, 0)
        dwd[last, pl.ds(pl.multiple_of(c * C, C), C)] = dot(hid[...], dy[...], 0, 0)

    load_a = pltpu.make_async_copy(a_hbm, a, local_sem.at[2])
    load_a.start()
    rs_step(False, chunks - 1, 0, True)
    rs_step(False, chunks - 2, 3)
    rs_step(True, last, 0)

    def norm_back(lo, hi):
        @pl.loop(lo, hi)
        def _(t):
            r = tile_rows(t)
            h = x[r].astype(F32)
            by_a = da[r].astype(BF).astype(F32)
            scale = lax.rsqrt(jnp.mean(h * h, -1, keepdims=True) + 1e-6)
            along = jnp.mean(h * by_a, -1, keepdims=True) * (scale * scale * scale)
            by_h = (by_a * scale - h * along).astype(BF)
            x[r] = (dy[r].astype(F32) + by_h.astype(F32)).astype(BF)

    norm_back(0, 2)
    rs_step(False, chunks - 1, 1)
    rs_final(False, chunks - 2, last, chunks - 2, True)
    norm_back(2, 4)
    rs_step(False, chunks - 1, 2)

    @pl.loop(0, chunks)
    def _(c):
        cols = pl.ds(pl.multiple_of(c * C, C), C)
        dwd[0, cols] = dot(hidden[:, cols], x[...], 0, 0)

    load_a.wait()

    @pl.loop(0, chunks)
    def _(c):
        half_0 = functools.partial(first_half, 0, c, back=x)

        @pl.when(c >= 1)
        def _():
            rs_step(False, chunks + c - 1, 0, c >= 1)

        @pl.when(c >= 2)
        def _():
            rs_step(False, chunks + c - 2, 3)

        @pl.when(c == 0)
        def _():
            rs_step(False, chunks - 1, 3)
            rs_step(True, 0, 0)

        half_0(t=0)

        @pl.when(c == 0)
        def _():
            rs_step(True, last, 1)

        @pl.when(c == 1)
        def _():
            rs_step(True, last, 3)

        @pl.when(c == 2)
        def _():
            rs_step(True, 0, 2)

        half_0(t=1)

        @pl.when(c >= 1)
        def _():
            rs_step(False, chunks + c - 1, 1)

        @pl.when(c >= 2)
        def _():
            rs_final(False, chunks + c - 2, 0, c - 2, c - 2 <= chunks - 3)

        @pl.when(c == 0)
        def _():
            rs_final(False, chunks - 1, last, chunks - 1, True)

        half_0(t=2)

        @pl.when(c == 1)
        def _():
            rs_step(True, 0, 1)

        @pl.when(c == 2)
        def _():
            rs_final(True, last, last, None)

        @pl.when(c == 3)
        def _():
            rs_step(True, 0, 3)

        half_0(t=3)

        @pl.when(c == 0)
        def _():
            rs_step(True, last, 2)

        @pl.when(c == 4)
        def _():
            rs_final(True, 0, 0, None)

        @pl.when(c >= 1)
        def _():
            rs_step(False, chunks + c - 1, 2)

        acc[lax.rem(chunks + c, 2)] = dot(a[...], dgu[...], 0, 0)

    s = 2 * chunks - 1
    rs_step(False, s, 0, True)
    rs_step(False, s - 1, 3)
    rs_step(False, s, 1)
    rs_final(False, s - 1, 0, chunks - 2)
    rs_step(False, s, 2)
    rs_step(False, s, 3)
    rs_final(False, s, 0, chunks - 1)

    total = jnp.sum(ss[...]) + jnp.sum(ssd[...])
    others[me] = jnp.full(others.shape[1:], total, F32)
    copies = []
    for off in range(1, n):
        copies.append(
            pltpu.make_async_remote_copy(
                src_ref=others.at[me], dst_ref=others.at[me], send_sem=sq_send.at[off], recv_sem=sq_recv.at[off],
                device_id={"dp": ring(off)}, device_id_type=MESH,
            )
        )
    for copy in copies:
        copy.start()
    for off in range(1, n):
        slot = others.at[ring(-off)]
        pltpu.make_async_copy(slot, slot, sq_recv.at[off]).wait()
    squares_ref[...] = jnp.sum(others[...], axis=0)
    for copy in copies:
        copy.wait_send()
    for u in range(len(units)):
        pltpu.make_async_copy(everything(u), everything(u), ag_send.at[u]).wait()
        pltpu.make_async_copy(everything(u), everything(u), pair_send.at[u]).wait()


def adamw_kernel(count, squares, *refs):
    factor = jnp.minimum(1.0, 0.5 * lax.rsqrt(squares[0:1, 0:1] / count + 1e-30))
    gs, ws, ms, vs, new_w, new_m, new_v = (refs[i : i + 3] for i in range(0, 21, 3))
    for i in range(3):
        g = gs[i][...].astype(F32) * factor
        m = 0.9 * ms[i][...] + 0.1 * g
        v = 0.95 * vs[i][...] + 0.05 * g * g
        w = ws[i][...].astype(F32)
        new_w[i][...] = (w - 0.02 * (m * lax.rsqrt(v + 1e-8) + 0.1 * w)).astype(BF)
        new_m[i][...] = m
        new_v[i][...] = v


def solution(mesh):
    n = mesh.shape["dp"]

    def step(x, dy, *arrays):
        weights, m, v = (arrays[i : i + 3] for i in (0, 3, 6))
        x, dy = x[0], dy[0]
        tokens, d_model = x.shape
        layers, rows_gu, ff = weights[0].shape
        rows_d = weights[2].shape[1]
        chunks = ff // C
        messages = 2 * (n - 1)
        hbm = pl.BlockSpec(memory_space=pl.ANY)
        vmem = pl.BlockSpec(memory_space=pltpu.VMEM)
        dma = pltpu.SemaphoreType.DMA
        gg, gu, gd, squares, _ = pl.pallas_call(
            functools.partial(step_kernel, n, layers, d_model, ff, tokens),
            out_shape=[jax.ShapeDtypeStruct(w.shape, BF) for w in weights]
            + [jax.ShapeDtypeStruct((8, 128), F32), jax.ShapeDtypeStruct((tokens, d_model), BF)],
            in_specs=[hbm] * 5,
            out_specs=[vmem] * 4 + [hbm],
            scratch_shapes=[
                pltpu.VMEM((tokens, d_model), BF),
                pltpu.VMEM((tokens, d_model), BF),
                pltpu.VMEM((tokens, d_model), BF),
                pltpu.VMEM((tokens, d_model), F32),
                pltpu.VMEM((tokens, ff), BF),
                pltpu.VMEM((layers, chunks, d_model, 2 * C), BF),
                pltpu.VMEM((layers, ff, d_model), BF),
                pltpu.VMEM((tokens, 2 * C), BF),
                pltpu.VMEM((tokens, C), BF),
                pltpu.VMEM((2, d_model, 2 * C), F32),
                pltpu.VMEM((layers, ff, d_model), F32),
                pltpu.VMEM((2, messages + 4, rows_gu, C), BF),
                pltpu.VMEM((layers, messages + 4, rows_d, d_model // 2), BF),
                pltpu.VMEM((rows_gu, C), F32),
                pltpu.VMEM((rows_d, d_model // 2), F32),
                pltpu.VMEM((n, 8, 128), F32),
                dma((3,)),
                dma((layers * (2 * chunks + 1),)),
                dma((7, messages)),
                dma((7,)),
                dma((7,)),
                dma((7,)),
                dma((2, messages)),
                dma((2,)),
                dma((layers, messages)),
                dma((layers,)),
                dma((n,)),
                dma((n,)),
                pltpu.SemaphoreType.REGULAR((2,)),
            ],
            compiler_params=pltpu.CompilerParams(collective_id=0, has_side_effects=True, vmem_limit_bytes=67043328),
            name="train_step",
        )(x, dy, *weights)

        cut = 2
        specs = [pl.BlockSpec((1, w.shape[1] // cut, w.shape[2]), lambda l, i: (l, i, 0)) for w in weights]
        out = pl.pallas_call(
            functools.partial(adamw_kernel, float(n * sum(w.size for w in weights))),
            grid=(layers, cut),
            out_shape=[jax.ShapeDtypeStruct(w.shape, dtype) for dtype in (BF, F32, F32) for w in weights],
            in_specs=[pl.BlockSpec((8, 128), lambda l, i: (0, 0))] + specs * 4,
            out_specs=specs * 3,
            name="adamw",
        )(squares, gg, gu, gd, *weights, *m, *v)
        return tuple(out)

    states, cut = P(("rep", "dp"), None, None), P(None, "dp", None)
    return jax.shard_map(
        step,
        mesh=mesh,
        in_specs=(states, states) + (cut,) * 9,
        out_specs=(P("rep", "dp", None),) * 9,
        check_vma=False,
    )
```

time: 555 us -> 220 us (0.40); the launches traced: 545 us -> 220 us
  waiting for transfers between devices: 254 us -> 0 us
  matrix products: 221 us -> 0 us
  Pallas kernels: 0 us -> 219 us
  local copies, waits for them, and re-layouts: 18.7 us -> 0 us
  other arithmetic: 17.5 us -> 0 us
  between operations: 17.6 us -> 0.83 us
  blocking collectives: 16.2 us -> 0 us
    dot_general x15 -> x0, matrix products: 221 us -> none  [the longest x5 82.1 us: layer(): gate = jnp.dot(a, w['w_gate'], preferred_element_type=jnp.float32)]
    pallas_call x0 -> x2, Pallas kernels: none -> 219 us  [the longest x1 214 us: step(): pl.pallas_call(functools.partial(step_kernel, n, layers, d_model, ff, tok...]
    all_gather x6 -> x0, waiting for transfers between devices: 134 us -> none  [fetched(): lax.all_gather(w[number], 'dp', axis=0, tiled=True)]
    reduce_scatter x6 -> x0, waiting for transfers between devices: 118 us -> none  [step(): lax.psum_scatter(by_w[name], 'dp', scatter_dimension=0, tiled=True)]
    psum x1 -> x0, blocking collectives: 16.2 us -> none  [step(): squares = lax.psum(sum((jnp.sum(g * g) for g in gradients)), 'dp')]
    unnamed x38 -> x0, local copies, waits for them, and re-layouts: 13.5 us -> none
    reduce_sum x4 -> x0, other arithmetic: 8.37 us -> none  [the longest x3 5.3 us: step(): squares = lax.psum(sum((jnp.sum(g * g) for g in gradients)), 'dp')]
    convert_element_type x2 -> x0, other arithmetic: 6.29 us -> none  [adamw(): return ((w - 0.02 * step).astype(jnp.bfloat16), m, v)]
  transfers between devices with their start and end apart: 12 -> 0, of which waited for: 10 -> 0; matrix products, arithmetic and copies ran while one was open for 38% -> 0% of each run, Pallas kernels for 0% -> 0%
where the time goes in v1:
time: 220 us
  Pallas kernels  219 us (100%)
    pallas_call x1, Pallas kernels, step(): pl.pallas_call(functools.partial(step_kernel, n, layers, d_model, ff, tok...  214 us
    pallas_call x1, Pallas kernels, step(): pl.pallas_call(functools.partial(adamw_kernel, float(n * sum((w.size for...  5.58 us

profile of v1, /device:TPU:22, one launch (start us, length us, event | category | flops | bytes accessed | tf_op | source)
XLA Modules:
  0.0 220.0 jit_solution(11166512216422607749)
XLA Ops:
  0.6 213.6 %train_step.1 = (bf16[2,64,1280]{2,1,0:T(8,128)(2,1)}, bf16[2,64,1280]{2,1,0:T(8,128)(2,1)}, bf16[2,160,512]{2,1,0:T(8,128)(2,1)}, f32[8,128]{1,0:T(8,128)}, bf16[4096,512]{1,0:T(8,128)(2,1)}) custom-call(bf16[4096,512]{1,0:T(8,128)(2,1)} %bitcast.2, bf16[4096,512]{1,0:T(8,128)(2,1)} %bitcast.3, bf16[2,64,1280]{2,1,0:T(8,128)(2,1)} %refs_3_.1, ...), custom_call_target="tpu_custom_call" | custom-call | tf_op jit(solution)/shard_map/train_step/pallas_call | solution.py:468
  214.2 5.6 %adamw.1 = (bf16[2,64,1280]{2,1,0:T(8,128)(2,1)}, bf16[2,64,1280]{2,1,0:T(8,128)(2,1)}, bf16[2,160,512]{2,1,0:T(8,128)(2,1)}, f32[2,64,1280]{2,1,0:T(8,128)}, f3...) custom-call(f32[8,128]{1,0:T(8,128)} %get-tuple-element.13.squares, ...), custom_call_target="tpu_custom_call" | custom-call | tf_op jit(solution)/shard_map/adamw/pallas_call | solution.py:511

commit v2 on v1

v2 whole, which is shorter than its diff:
```python
import functools

import jax
import jax.numpy as jnp
from jax import lax
from jax.experimental import pallas as pl
from jax.experimental.pallas import tpu as pltpu
from jax.sharding import PartitionSpec as P

BF, F32 = jnp.bfloat16, jnp.float32
C = 256
TILES = 4
A, B = 0, 1
RIGHT, LEFT = 0, 1


def dot(a, b, ca=1, cb=0):
    return lax.dot_general(a, b, (((ca,), (cb,)), ((), ())), preferred_element_type=F32)


def sigmoid(g):
    return 0.5 * jnp.tanh(0.5 * g) + 0.5


def normed(h):
    return (h * lax.rsqrt(jnp.mean(h * h, -1, keepdims=True) + 1e-6)).astype(BF)


def await_bytes(ref, sem):
    pltpu.make_async_copy(ref, ref, sem).wait()


def when(condition):
    return (lambda body: body()) if condition is True else pl.when(condition)


def routes(n):
    far, near = n // 2, n - 1 - n // 2
    hops = {(A, RIGHT): far, (A, LEFT): near, (B, RIGHT): near, (B, LEFT): far}
    number, k = {}, 0
    for (m, d), count in hops.items():
        for hop in range(1, count + 1):
            number[m, d, hop] = k
            k += 1
    return hops, number, k


def dealt(w, n):
    ff = w.shape[-1]
    owned, part = ff // n, C // n
    pieces = [w[:, z * owned + j * part : z * owned + (j + 1) * part] for j in range(ff // C) for z in range(n)]
    return jnp.concatenate(pieces, axis=1)


def gathered_back(w, n):
    ff = w.shape[-1]
    part = C // n
    pieces = [w[:, j * C + z * part : j * C + (z + 1) * part] for z in range(n) for j in range(ff // C)]
    return jnp.concatenate(pieces, axis=1)


def step_kernel(
    n, layers, d_model, ff, tokens, units,
    x_hbm, dy_hbm, wg_hbm, wu_hbm, wd_hbm,
    gg_ref, gu_ref, gd_ref, squares_ref, a_hbm,
    x, a, dy, da, hidden, wgu, wd, dgu, hid, acc, buf, ss, others, raw,
    local_sem, own_sem, ag_recv, ag_send, pair_recv, pair_send, side_recv, side_send, rs_recv, rs_send, sq_recv, sq_send, credit,
):
    me, rep = lax.axis_index("dp"), lax.axis_index("rep")
    core, row = lax.rem(rep, 2), lax.rem(rep // 2, 2)
    partner = {"rep": rep + 1 - 2 * core}
    beside = {"rep": rep + 2 - 4 * row}
    ring = lambda off: lax.rem(me + off + n, n)
    to = {RIGHT: {"dp": ring(1)}, LEFT: {"dp": ring(-1)}}
    sign = {RIGHT: 1, LEFT: -1}
    hops, number, messages = routes(n)
    chunks = ff // C
    rows_gu, rows_d = d_model // n, C // n
    half_gu, half_d = rows_gu // 2, rows_d // 2
    half_w = d_model // 2
    tile = tokens // TILES
    MESH = pl.DeviceIdType.MESH

    barrier = pltpu.get_barrier_semaphore()
    for off in range(1, n):
        pl.semaphore_signal(barrier, inc=1, device_id={"dp": ring(off)}, device_id_type=MESH)
    pl.semaphore_signal(barrier, inc=1, device_id=partner, device_id_type=MESH)
    pl.semaphore_signal(barrier, inc=1, device_id=beside, device_id_type=MESH)
    mine_gu = pl.ds(pl.multiple_of(me * rows_gu, rows_gu), rows_gu)
    mine_d = pl.ds(pl.multiple_of(me * rows_d, rows_d), rows_d)
    own = [(wg_hbm, raw.at[0]), (wu_hbm, raw.at[1])]
    for l in range(layers):
        for c in range(chunks):
            own.append((wd_hbm.at[l, pl.ds(c * rows_d, rows_d)], wd.at[l, c, mine_d]))
    own = [pltpu.make_async_copy(s, t, own_sem.at[i]) for i, (s, t) in enumerate(own)]
    for copy in own:
        copy.start()
    load_x = pltpu.make_async_copy(x_hbm, x, local_sem.at[0])
    load_dy = pltpu.make_async_copy(dy_hbm, dy, local_sem.at[1])
    load_x.start()
    load_dy.start()
    own[0].wait()
    own[1].wait()

    def deal(l):
        for m in range(2):
            block = dealt(raw[m, l].astype(F32), n).astype(BF)
            for c in range(chunks):
                wgu[l, c, mine_gu, pl.ds(m * C, C)] = block[:, c * C : (c + 1) * C]

    deal(0)
    pl.semaphore_wait(barrier, n + 1)
    for copy in own[2:]:
        copy.wait()

    def region(u, owner, first, width):
        l, down, c, count = units[u]
        if down:
            rows = pl.ds(pl.multiple_of(owner * rows_d + core * half_d, half_d), half_d)
            return wd.at[l, pl.ds(c, count), rows, pl.ds(first, width)]
        rows = pl.ds(pl.multiple_of(owner * rows_gu + core * half_gu, half_gu), half_gu)
        return wgu.at[l, pl.ds(c, count), rows, pl.ds(pl.multiple_of(first, 128), width)]

    def piece(u, m, owner):
        if units[u][1]:
            return region(u, owner, m * half_w, half_w)
        return region(u, owner, row * C + m * (C // 2), C // 2)

    def amount(u, both=False):
        l, down, c, count = units[u]
        if down:
            return wd.at[l, pl.ds(c, count), pl.ds(0, messages * half_d // 2), pl.ds(0, 2 * half_w)]
        return wgu.at[l, pl.ds(c, count), pl.ds(0, messages * half_gu // 2), pl.ds(0, 2 * C if both else C)]

    def send(block, send_sem, recv_sem, device):
        pltpu.make_async_remote_copy(
            src_ref=block, dst_ref=block, send_sem=send_sem, recv_sem=recv_sem, device_id=device, device_id_type=MESH
        ).start()

    def gather(u, k):
        for (m, d), count in hops.items():
            if k > count:
                continue
            block = piece(u, m, ring(-sign[d] * k))
            if k:
                await_bytes(block, ag_recv.at[u, number[m, d, k]])
            if k < count:
                send(block, ag_send.at[u], ag_recv.at[u, number[m, d, k + 1]], to[d])
            if k:
                if not units[u][1]:
                    send(block, side_send.at[u], side_recv.at[u], beside)
                send(block, pair_send.at[u], pair_recv.at[u], partner)

    def pass_on(u):
        await_bytes(amount(u), side_recv.at[u])
        for off in range(1, n):
            send(region(u, ring(off), (1 - row) * C, C), pair_send.at[u], pair_recv.at[u], partner)

    def gathered(u):
        await_bytes(amount(u, True), pair_recv.at[u])

    def rs_at(s):
        slot = lax.rem(s, 3)
        return acc.at[slot], buf.at[slot], slot

    def rs_term(total, owner, m):
        cols = pl.ds(m * C, C)
        gu = total[pl.ds(pl.multiple_of(owner * rows_gu, rows_gu), rows_gu), cols]
        down = total[pl.ds(pl.multiple_of(d_model + owner * rows_d, rows_d), rows_d), cols]
        return jnp.concatenate([gu, down], axis=0)

    def rs_step(s, k, wait_credit=None):
        total, slots, slot = rs_at(s)
        if wait_credit is not None:

            @when(wait_credit)
            def _():
                pl.semaphore_wait(credit.at[0], 1)
                pl.semaphore_wait(credit.at[1], 1)

        out = []
        for i, ((m, d), count) in enumerate(hops.items()):
            if k >= count:
                continue
            term = rs_term(total, ring(sign[d] * (count - k)), m)
            if k == 0:
                at = messages + i
            else:
                at = number[m, d, k]
                await_bytes(slots.at[at], rs_recv.at[slot, at])
                term = term + slots[at].astype(F32)
            slots[at] = term.astype(BF)
            out.append((m, d, at))
        for m, d, at in out:
            there = number[m, d, k + 1]
            pltpu.make_async_remote_copy(
                src_ref=slots.at[at], dst_ref=slots.at[there], send_sem=rs_send.at[slot], recv_sem=rs_recv.at[slot, there],
                device_id=to[d], device_id_type=MESH,
            ).start()

    def rs_final(s, l, c, give=None):
        total, slots, slot = rs_at(s)
        for m in (A, B):
            g = rs_term(total, me, m)
            for d in (RIGHT, LEFT):
                at = number[m, d, hops[m, d]]
                await_bytes(slots.at[at], rs_recv.at[slot, at])
                g = g + slots[at].astype(F32)
            g = g.astype(BF)
            (gg_ref, gu_ref)[m][l, :, pl.ds(pl.multiple_of(c * C, C), C)] = g[:rows_gu]
            gd_ref[l, pl.ds(pl.multiple_of(c * rows_d, rows_d), rows_d), pl.ds(m * half_w, half_w)] = g[rows_gu:]
            wide = g.astype(F32)
            ss[...] += wide * wide
        await_bytes(slots.at[pl.ds(0, messages)], rs_send.at[slot])
        if give is not None:

            @when(give)
            def _():
                pl.semaphore_signal(credit.at[0], inc=1, device_id=to[LEFT], device_id_type=MESH)
                pl.semaphore_signal(credit.at[1], inc=1, device_id=to[RIGHT], device_id_type=MESH)

    def tile_rows(t):
        return pl.ds(pl.multiple_of(t * tile, tile), tile)

    def first_norm(lo, hi):
        @pl.loop(lo, hi)
        def _(t):
            r = tile_rows(t)
            a[r] = normed(x[r].astype(F32))

    gather(0, 0)
    gather(1, 0)
    ss[...] = jnp.zeros_like(ss)
    load_x.wait()
    first_norm(0, 2)
    gather(0, 1)
    gather(1, 1)
    gather(2, 0)
    first_norm(2, 4)
    save_a = pltpu.make_async_copy(a, a_hbm, local_sem.at[2])
    save_a.start()
    gather(0, 2)
    gather(1, 2)
    gather(2, 1)
    deal(1)
    da[...] = jnp.zeros_like(da)
    gather(0, 3)
    gather(0, 4)
    gather(1, 3)
    gather(2, 2)
    gather(3, 0)
    load_dy.wait()
    pass_on(0)
    gathered(0)

    before = {
        1: [(1, 4), (2, 3), (3, 1)],
        2: [(2, 4), (3, 2), (4, 0)],
        3: [(3, 3), (4, 1), (5, 0)],
        4: [(3, 4), (4, 2), (5, 1)],
    }
    for c in range(chunks):
        for event in before.get(c, ()):
            gather(*event)
        if c == 1:
            pass_on(1)
            gathered(1)
        if c == 2:
            pass_on(2)
        if c == 3:
            gathered(2)

        @pl.loop(0, TILES)
        def _(t):
            r = tile_rows(t)
            both = dot(a[r], wgu[0, c])
            g, u = both[:, :C], both[:, C:]
            hidden[r, c * C : (c + 1) * C] = (g * sigmoid(g) * u).astype(BF)

    gather(4, 3)
    gather(5, 2)
    gathered(3)
    save_a.wait()
    between = {0: [], 1: [(4, 4), (5, 3)], 2: [(5, 4)], 3: []}
    for t in range(TILES):
        for event in between[t]:
            gather(*event)
        if t == 2:
            pass_on(4)
        r = pl.ds(t * tile, tile)
        out = dot(hidden[r], wd[0].reshape(ff, d_model)).astype(BF)
        h = (x[r].astype(F32) + out.astype(F32)).astype(BF)
        x[r] = h
        a[r] = normed(h.astype(F32))
    for u in (4, 5):
        gathered(u)

    def tile_back(l, c, t, back):
        r = tile_rows(t)
        both = dot(a[r], wgu[l, c])
        g, u = both[:, :C], both[:, C:]
        dh = dot(back[r], wd[l, c], 1, 1).astype(BF).astype(F32)
        s = sigmoid(g)
        silu = g * s
        slope = s + silu * (1.0 - s)
        both = jnp.concatenate([(dh * u * slope).astype(BF), (dh * silu).astype(BF)], axis=1)
        dgu[r] = both
        hid[r] = (silu * u).astype(BF)
        if l == layers - 1:
            da[r] += dot(both, wgu[l, c], 1, 1)

    last = layers - 1

    def layer_back(l, s0, back, early):
        give = lambda s: s <= layers * chunks - 4

        @pl.loop(0, chunks)
        def _(c):
            slot = lax.rem(s0 + c, 3)
            early(c, 0)

            @pl.when(c >= 1)
            def _():
                rs_step(s0 + c - 1, 0, s0 + c - 1 >= 3)

            @pl.when(c >= 2)
            def _():
                rs_step(s0 + c - 2, 2)

            @pl.when(c >= 3)
            def _():
                rs_final(s0 + c - 3, l, c - 3, give(s0 + c - 3))

            tile_back(l, c, 0, back)
            tile_back(l, c, 1, back)
            tile_back(l, c, 2, back)
            tile_back(l, c, 3, back)
            early(c, 1)

            @pl.when(c >= 1)
            def _():
                rs_step(s0 + c - 1, 1)

            @pl.when(c >= 2)
            def _():
                rs_step(s0 + c - 2, 3)

            acc[slot, :d_model] = dot(a[...], dgu[...], 0, 0)
            acc[slot, d_model:] = dot(hid[...], back[...], 0, 0)

    layer_back(last, 0, dy, lambda c, point: None)

    load_a = pltpu.make_async_copy(a_hbm, a, local_sem.at[2])
    load_a.start()
    s = chunks - 1
    rs_step(s, 0, True)
    rs_step(s - 1, 2)
    rs_final(s - 2, last, chunks - 3, True)

    @pl.loop(0, TILES)
    def _(t):
        r = tile_rows(t)
        h = x[r].astype(F32)
        by_a = da[r].astype(BF).astype(F32)
        scale = lax.rsqrt(jnp.mean(h * h, -1, keepdims=True) + 1e-6)
        along = jnp.mean(h * by_a, -1, keepdims=True) * (scale * scale * scale)
        by_h = (by_a * scale - h * along).astype(BF)
        x[r] = (dy[r].astype(F32) + by_h.astype(F32)).astype(BF)

    rs_step(s, 1)
    rs_step(s - 1, 3)
    load_a.wait()

    def early(c, point):
        @pl.when(c == 0)
        def _():
            if point == 0:
                rs_step(s, 2)
                rs_final(s - 1, last, chunks - 2, True)
            else:
                rs_step(s, 3)

        if point == 0:

            @pl.when(c == 1)
            def _():
                rs_final(s, last, chunks - 1, True)

    layer_back(0, chunks, x, early)

    s = layers * chunks - 1
    rs_step(s, 0, True)
    rs_step(s - 1, 2)
    rs_final(s - 2, 0, chunks - 3)
    rs_step(s, 1)
    rs_step(s - 1, 3)
    rs_step(s, 2)
    rs_final(s - 1, 0, chunks - 2)
    rs_step(s, 3)
    rs_final(s, 0, chunks - 1)

    others[me] = jnp.full(others.shape[1:], jnp.sum(ss[...]), F32)
    copies = []
    for off in range(1, n):
        copies.append(
            pltpu.make_async_remote_copy(
                src_ref=others.at[me], dst_ref=others.at[me], send_sem=sq_send.at[off], recv_sem=sq_recv.at[off],
                device_id={"dp": ring(off)}, device_id_type=MESH,
            )
        )
    for copy in copies:
        copy.start()
    for off in range(1, n):
        slot = others.at[ring(-off)]
        await_bytes(slot, sq_recv.at[off])
    squares_ref[...] = jnp.sum(others[...], axis=0)
    for copy in copies:
        copy.wait_send()
    for u in range(len(units)):
        await_bytes(amount(u), ag_send.at[u])
        await_bytes(amount(u, True), pair_send.at[u])
        if not units[u][1]:
            await_bytes(amount(u), side_send.at[u])


def adamw_kernel(n, count, squares, *refs):
    factor = jnp.minimum(1.0, 0.5 * lax.rsqrt(squares[0:1, 0:1] / count + 1e-30))
    gs, ws, ms, vs, new_w, new_m, new_v = (refs[i : i + 3] for i in range(0, 21, 3))
    for i in range(3):
        g = gs[i][0].astype(F32) * factor
        g = (g if i == 2 else gathered_back(g, n))[None]
        m = 0.9 * ms[i][...] + 0.1 * g
        v = 0.95 * vs[i][...] + 0.05 * g * g
        w = ws[i][...].astype(F32)
        new_w[i][...] = (w - 0.02 * (m * lax.rsqrt(v + 1e-8) + 0.1 * w)).astype(BF)
        new_m[i][...] = m
        new_v[i][...] = v


def solution(mesh):
    n = mesh.shape["dp"]

    def step(x, dy, *arrays):
        weights, m, v = (arrays[i : i + 3] for i in (0, 3, 6))
        x, dy = x[0], dy[0]
        tokens, d_model = x.shape
        layers, rows_gu, ff = weights[0].shape
        chunks = ff // C
        messages = 2 * (n - 1)
        hbm = pl.BlockSpec(memory_space=pl.ANY)
        vmem = pl.BlockSpec(memory_space=pltpu.VMEM)
        dma = pltpu.SemaphoreType.DMA
        units = [(0, False, 0, 1), (0, False, 1, 2), (0, False, 3, chunks - 3), (0, True, 0, chunks)]
        units += [(1, False, 0, chunks), (1, True, 0, chunks)]
        gg, gu, gd, squares, _ = pl.pallas_call(
            functools.partial(step_kernel, n, layers, d_model, ff, tokens, units),
            out_shape=[jax.ShapeDtypeStruct(w.shape, BF) for w in weights]
            + [jax.ShapeDtypeStruct((8, 128), F32), jax.ShapeDtypeStruct((tokens, d_model), BF)],
            in_specs=[hbm] * 5,
            out_specs=[vmem] * 4 + [hbm],
            scratch_shapes=[
                pltpu.VMEM((tokens, d_model), BF),
                pltpu.VMEM((tokens, d_model), BF),
                pltpu.VMEM((tokens, d_model), BF),
                pltpu.VMEM((tokens, d_model), F32),
                pltpu.VMEM((tokens, ff), BF),
                pltpu.VMEM((layers, chunks, d_model, 2 * C), BF),
                pltpu.VMEM((layers, chunks, C, d_model), BF),
                pltpu.VMEM((tokens, 2 * C), BF),
                pltpu.VMEM((tokens, C), BF),
                pltpu.VMEM((3, d_model + C, 2 * C), F32),
                pltpu.VMEM((3, messages + 4, rows_gu + C // n, C), BF),
                pltpu.VMEM((rows_gu + C // n, C), F32),
                pltpu.VMEM((n, 8, 128), F32),
                pltpu.VMEM((2,) + weights[0].shape, BF),
                dma((3,)),
                dma((2 + layers * chunks,)),
                dma((len(units), messages)),
                dma((len(units),)),
                dma((len(units),)),
                dma((len(units),)),
                dma((len(units),)),
                dma((len(units),)),
                dma((3, messages)),
                dma((3,)),
                dma((n,)),
                dma((n,)),
                pltpu.SemaphoreType.REGULAR((2,)),
            ],
            compiler_params=pltpu.CompilerParams(collective_id=0, has_side_effects=True, vmem_limit_bytes=67043328),
            name="train_step",
        )(x, dy, *weights)

        cut = 2
        specs = [pl.BlockSpec((1, w.shape[1] // cut, w.shape[2]), lambda l, i: (l, i, 0)) for w in weights]
        out = pl.pallas_call(
            functools.partial(adamw_kernel, n, float(n * sum(w.size for w in weights))),
            grid=(layers, cut),
            out_shape=[jax.ShapeDtypeStruct(w.shape, dtype) for dtype in (BF, F32, F32) for w in weights],
            in_specs=[pl.BlockSpec((8, 128), lambda l, i: (0, 0))] + specs * 4,
            out_specs=specs * 3,
            name="adamw",
        )(squares, gg, gu, gd, *weights, *m, *v)
        return tuple(out)

    states, cut = P(("rep", "dp"), None, None), P(None, "dp", None)
    return jax.shard_map(
        step,
        mesh=mesh,
        in_specs=(states, states) + (cut,) * 9,
        out_specs=(P("rep", "dp", None),) * 9,
        check_vma=False,
    )
```

time: 220 us -> 205 us (0.932)
  Pallas kernels: 219 us -> 204 us
    pallas_call x1, Pallas kernels: 214 us -> 199 us  [step(): pl.pallas_call(functools.partial(step_kernel, n, layers, d_model, ff, tok...]
where the time goes in v2:
time: 205 us
  Pallas kernels  204 us (100%)
    pallas_call x1, Pallas kernels, step(): pl.pallas_call(functools.partial(step_kernel, n, layers, d_model, ff, tok...  199 us
    pallas_call x1, Pallas kernels, step(): pl.pallas_call(functools.partial(adamw_kernel, n, float(n * sum((w.size f...  5.74 us

profile of v2, /device:TPU:22, one launch (start us, length us, event | category | flops | bytes accessed | tf_op | source)
XLA Modules:
  0.0 205.2 jit_solution(2013475397993303732)
XLA Ops:
  0.6 198.6 %train_step.1 = (bf16[2,64,1280]{2,1,0:T(8,128)(2,1)}, bf16[2,64,1280]{2,1,0:T(8,128)(2,1)}, bf16[2,160,512]{2,1,0:T(8,128)(2,1)}, f32[8,128]{1,0:T(8,128)}, bf16[4096,512]{1,0:T(8,128)(2,1)}) custom-call(bf16[4096,512]{1,0:T(8,128)(2,1)} %bitcast.2, bf16[4096,512]{1,0:T(8,128)(2,1)} %bitcast.3, bf16[2,64,1280]{2,1,0:T(8,128)(2,1)} %refs_3_.1, ...), custom_call_target="tpu_custom_call" | custom-call | tf_op jit(solution)/shard_map/train_step/pallas_call | solution.py:455
  199.2 5.7 %adamw.1 = (bf16[2,64,1280]{2,1,0:T(8,128)(2,1)}, bf16[2,64,1280]{2,1,0:T(8,128)(2,1)}, bf16[2,160,512]{2,1,0:T(8,128)(2,1)}, f32[2,64,1280]{2,1,0:T(8,128)}, f3...) custom-call(f32[8,128]{1,0:T(8,128)} %get-tuple-element.13.squares, ...), custom_call_target="tpu_custom_call" | custom-call | tf_op jit(solution)/shard_map/adamw/pallas_call | solution.py:496

commit v3 on v2

--- a/solution.py
+++ b/solution.py
@@ -62,9 +62,9 @@
 def step_kernel(
     n, layers, d_model, ff, tokens, units,
     x_hbm, dy_hbm, wg_hbm, wu_hbm, wd_hbm,
-    gg_ref, gu_ref, gd_ref, squares_ref, a_hbm,
-    x, a, dy, da, hidden, wgu, wd, dgu, hid, acc, buf, ss, others, raw,
-    local_sem, own_sem, ag_recv, ag_send, pair_recv, pair_send, side_recv, side_send, rs_recv, rs_send, sq_recv, sq_send, credit,
+    gg_hbm, gu_hbm, gd_hbm, squares_ref, a_hbm,
+    x, a, dy, da, hidden, wgu, wd, dgu, hid, acc, buf, ss, others, raw, gg_ref, gu_ref, gd_ref,
+    local_sem, own_sem, ag_recv, ag_send, pair_recv, pair_send, side_recv, side_send, rs_recv, rs_last, rs_send, sq_recv, sq_send, credit,
 ):
     me, rep = lax.axis_index("dp"), lax.axis_index("rep")
     core, row = lax.rem(rep, 2), lax.rem(rep // 2, 2)
@@ -151,6 +151,17 @@
                     send(block, side_send.at[u], side_recv.at[u], beside)
                 send(block, pair_send.at[u], pair_recv.at[u], partner)
 
+    def straight(u):
+        for off in sorted(range(1, n), key=lambda off: -min(off, n - off)):
+            send(region(u, me, row * C, C), ag_send.at[u], ag_recv.at[u, off], {"dp": ring(off)})
+
+    def straight_in(u):
+        for off in sorted(range(1, n), key=lambda off: min(off, n - off)):
+            block = region(u, ring(-off), row * C, C)
+            await_bytes(block, ag_recv.at[u, off])
+            send(block, side_send.at[u], side_recv.at[u], beside)
+            send(block, pair_send.at[u], pair_recv.at[u], partner)
+
     def pass_on(u):
         await_bytes(amount(u), side_recv.at[u])
         for off in range(1, n):
@@ -159,18 +170,26 @@
     def gathered(u):
         await_bytes(amount(u, True), pair_recv.at[u])
 
-    def rs_at(s):
+    whole = (0, rows_gu + rows_d)
+    parts = ((0, rows_gu), (rows_gu, rows_d))
+
+    def rs_at(s, part):
         slot = lax.rem(s, 3)
-        return acc.at[slot], buf.at[slot], slot
-
-    def rs_term(total, owner, m):
+        return acc.at[slot], buf.at[slot], slot, rs_recv.at[slot] if part is whole else rs_last.at[parts.index(part)]
+
+    def rs_term(total, owner, m, part):
         cols = pl.ds(m * C, C)
-        gu = total[pl.ds(pl.multiple_of(owner * rows_gu, rows_gu), rows_gu), cols]
-        down = total[pl.ds(pl.multiple_of(d_model + owner * rows_d, rows_d), rows_d), cols]
-        return jnp.concatenate([gu, down], axis=0)
-
-    def rs_step(s, k, wait_credit=None):
-        total, slots, slot = rs_at(s)
+        gu = pl.ds(pl.multiple_of(owner * rows_gu, rows_gu), rows_gu)
+        down = pl.ds(pl.multiple_of(d_model + owner * rows_d, rows_d), rows_d)
+        if part is whole:
+            return jnp.concatenate([total[gu, cols], total[down, cols]], axis=0)
+        return total[down if part[0] else gu, cols]
+
+    routes_far = (((A, RIGHT), (B, LEFT)), ((A, LEFT), (B, RIGHT)))
+
+    def rs_step(s, k, wait_credit=None, part=whole, groups=routes_far):
+        total, slots, slot, recv = rs_at(s, part)
+        rows = pl.ds(*part)
         if wait_credit is not None:
 
             @when(wait_credit)
@@ -178,39 +197,46 @@
                 pl.semaphore_wait(credit.at[0], 1)
                 pl.semaphore_wait(credit.at[1], 1)
 
-        out = []
-        for i, ((m, d), count) in enumerate(hops.items()):
-            if k >= count:
-                continue
-            term = rs_term(total, ring(sign[d] * (count - k)), m)
-            if k == 0:
-                at = messages + i
-            else:
-                at = number[m, d, k]
-                await_bytes(slots.at[at], rs_recv.at[slot, at])
-                term = term + slots[at].astype(F32)
-            slots[at] = term.astype(BF)
-            out.append((m, d, at))
-        for m, d, at in out:
-            there = number[m, d, k + 1]
-            pltpu.make_async_remote_copy(
-                src_ref=slots.at[at], dst_ref=slots.at[there], send_sem=rs_send.at[slot], recv_sem=rs_recv.at[slot, there],
-                device_id=to[d], device_id_type=MESH,
-            ).start()
-
-    def rs_final(s, l, c, give=None):
-        total, slots, slot = rs_at(s)
+        for group in groups:
+            out = []
+            for i, (m, d) in enumerate(group):
+                count = hops[m, d]
+                if k >= count:
+                    continue
+                term = rs_term(total, ring(sign[d] * (count - k)), m, part)
+                if k == 0:
+                    at = messages + 2 * routes_far.index(group) + i
+                else:
+                    at = number[m, d, k]
+                    await_bytes(slots.at[at, rows], recv.at[at])
+                    term = term + slots[at, rows].astype(F32)
+                slots[at, rows] = term.astype(BF)
+                out.append((m, d, at))
+            for m, d, at in out:
+                there = number[m, d, k + 1]
+                pltpu.make_async_remote_copy(
+                    src_ref=slots.at[at, rows], dst_ref=slots.at[there, rows], send_sem=rs_send.at[slot], recv_sem=recv.at[there],
+                    device_id=to[d], device_id_type=MESH,
+                ).start()
+
+    def rs_final(s, l, c, give=None, last_parts=(whole,)):
         for m in (A, B):
-            g = rs_term(total, me, m)
-            for d in (RIGHT, LEFT):
-                at = number[m, d, hops[m, d]]
-                await_bytes(slots.at[at], rs_recv.at[slot, at])
-                g = g + slots[at].astype(F32)
-            g = g.astype(BF)
-            (gg_ref, gu_ref)[m][l, :, pl.ds(pl.multiple_of(c * C, C), C)] = g[:rows_gu]
-            gd_ref[l, pl.ds(pl.multiple_of(c * rows_d, rows_d), rows_d), pl.ds(m * half_w, half_w)] = g[rows_gu:]
-            wide = g.astype(F32)
-            ss[...] += wide * wide
+            for part in last_parts:
+                total, slots, slot, recv = rs_at(s, part)
+                rows = pl.ds(*part)
+                g = rs_term(total, me, m, part)
+                for d in (RIGHT, LEFT):
+                    at = number[m, d, hops[m, d]]
+                    await_bytes(slots.at[at, rows], recv.at[at])
+                    g = g + slots[at, rows].astype(F32)
+                g = g.astype(BF)
+                if part[0] == 0:
+                    (gg_ref, gu_ref)[m][l, :, pl.ds(pl.multiple_of(c * C, C), C)] = g[:rows_gu]
+                if part[0] or part is whole:
+                    down = g[rows_gu:] if part is whole else g
+                    gd_ref[l, pl.ds(pl.multiple_of(c * rows_d, rows_d), rows_d), pl.ds(m * half_w, half_w)] = down
+                wide = g.astype(F32)
+                ss[rows] += wide * wide
         await_bytes(slots.at[pl.ds(0, messages)], rs_send.at[slot])
         if give is not None:
 
@@ -228,72 +254,67 @@
             r = tile_rows(t)
             a[r] = normed(x[r].astype(F32))
 
-    gather(0, 0)
-    gather(1, 0)
+    gather(2, 0)
+    straight(0)
+    straight(1)
     ss[...] = jnp.zeros_like(ss)
     load_x.wait()
     first_norm(0, 2)
-    gather(0, 1)
-    gather(1, 1)
-    gather(2, 0)
+    gather(2, 1)
     first_norm(2, 4)
     save_a = pltpu.make_async_copy(a, a_hbm, local_sem.at[2])
     save_a.start()
-    gather(0, 2)
-    gather(1, 2)
-    gather(2, 1)
+    straight_in(0)
+    gather(3, 0)
     deal(1)
     da[...] = jnp.zeros_like(da)
-    gather(0, 3)
-    gather(0, 4)
-    gather(1, 3)
     gather(2, 2)
-    gather(3, 0)
+    straight_in(1)
+    gather(4, 0)
     load_dy.wait()
     pass_on(0)
     gathered(0)
 
-    before = {
-        1: [(1, 4), (2, 3), (3, 1)],
-        2: [(2, 4), (3, 2), (4, 0)],
-        3: [(3, 3), (4, 1), (5, 0)],
-        4: [(3, 4), (4, 2), (5, 1)],
+    def ready(*us):
+        for u in us:
+            gathered(u)
+
+    meanwhile = {
+        1: lambda: (gather(2, 3), gather(3, 1)),
+        2: lambda: (pass_on(1), gather(5, 0), ready(1)),
+        3: lambda: (gather(2, 4), gather(4, 1)),
+        4: lambda: (gather(3, 2), pass_on(2), ready(2)),
+        5: lambda: gather(5, 1),
+        6: lambda: gather(4, 2),
+        7: lambda: gather(3, 3),
+        8: lambda: gather(5, 2),
+        9: lambda: (gather(4, 3), gather(3, 4)),
+        10: lambda: (save_a.wait(), ready(3)),
+        11: lambda: (gather(4, 4), gather(5, 3)),
+        13: lambda: (pass_on(4), gather(5, 4)),
+        14: lambda: ready(4, 5),
     }
-    for c in range(chunks):
-        for event in before.get(c, ()):
-            gather(*event)
-        if c == 1:
-            pass_on(1)
-            gathered(1)
-        if c == 2:
-            pass_on(2)
-        if c == 3:
-            gathered(2)
-
-        @pl.loop(0, TILES)
+    for point in range(2 * chunks):
+        if point in meanwhile:
+            meanwhile[point]()
+        c, lo = point // 2, point % 2 * 2
+
+        @pl.loop(lo, lo + 2)
         def _(t):
             r = tile_rows(t)
             both = dot(a[r], wgu[0, c])
             g, u = both[:, :C], both[:, C:]
             hidden[r, c * C : (c + 1) * C] = (g * sigmoid(g) * u).astype(BF)
 
-    gather(4, 3)
-    gather(5, 2)
-    gathered(3)
-    save_a.wait()
-    between = {0: [], 1: [(4, 4), (5, 3)], 2: [(5, 4)], 3: []}
     for t in range(TILES):
-        for event in between[t]:
-            gather(*event)
-        if t == 2:
-            pass_on(4)
+        if 2 * chunks + t in meanwhile:
+            meanwhile[2 * chunks + t]()
         r = pl.ds(t * tile, tile)
         out = dot(hidden[r], wd[0].reshape(ff, d_model)).astype(BF)
         h = (x[r].astype(F32) + out.astype(F32)).astype(BF)
         x[r] = h
         a[r] = normed(h.astype(F32))
-    for u in (4, 5):
-        gathered(u)
+    meanwhile[2 * chunks + TILES]()
 
     def tile_back(l, c, t, back):
         r = tile_rows(t)
@@ -306,98 +327,110 @@
         both = jnp.concatenate([(dh * u * slope).astype(BF), (dh * silu).astype(BF)], axis=1)
         dgu[r] = both
         hid[r] = (silu * u).astype(BF)
+
+    def add_da(l, c, t):
         if l == layers - 1:
-            da[r] += dot(both, wgu[l, c], 1, 1)
+            r = tile_rows(t)
+            da[r] += dot(dgu[r], wgu[l, c], 1, 1)
 
     last = layers - 1
 
+    final_stream = layers * chunks - 1
+
     def layer_back(l, s0, back, early):
-        give = lambda s: s <= layers * chunks - 4
+        give = lambda s: s <= final_stream - 3
 
         @pl.loop(0, chunks)
         def _(c):
             slot = lax.rem(s0 + c, 3)
-            early(c, 0)
+
+            def steps(point):
+                for (chunk, at), step in early.items():
+                    if at == point:
+                        pl.when(c == chunk)(step)
 
             @pl.when(c >= 1)
             def _():
                 rs_step(s0 + c - 1, 0, s0 + c - 1 >= 3)
-
-            @pl.when(c >= 2)
-            def _():
-                rs_step(s0 + c - 2, 2)
-
-            @pl.when(c >= 3)
-            def _():
-                rs_final(s0 + c - 3, l, c - 3, give(s0 + c - 3))
 
             tile_back(l, c, 0, back)
             tile_back(l, c, 1, back)
+            add_da(l, c, 0)
+            steps(1)
+
+            @pl.when(c >= 2)
+            def _():
+                rs_step(s0 + c - 2, 3)
+
             tile_back(l, c, 2, back)
+            add_da(l, c, 1)
+            steps(2)
+
+            @pl.when(c >= 1)
+            def _():
+                rs_step(s0 + c - 1, 1)
+
             tile_back(l, c, 3, back)
-            early(c, 1)
+            add_da(l, c, 2)
+
+            @pl.when(c >= 2)
+            def _():
+                rs_final(s0 + c - 2, l, c - 2, give(s0 + c - 2))
+
+            add_da(l, c, 3)
+            acc[slot, :d_model] = dot(a[...], dgu[...], 0, 0)
+            steps(4)
 
             @pl.when(c >= 1)
             def _():
-                rs_step(s0 + c - 1, 1)
-
-            @pl.when(c >= 2)
-            def _():
-                rs_step(s0 + c - 2, 3)
-
-            acc[slot, :d_model] = dot(a[...], dgu[...], 0, 0)
+                rs_step(s0 + c - 1, 2)
+
             acc[slot, d_model:] = dot(hid[...], back[...], 0, 0)
 
-    layer_back(last, 0, dy, lambda c, point: None)
+    layer_back(last, 0, dy, {})
 
     load_a = pltpu.make_async_copy(a_hbm, a, local_sem.at[2])
     load_a.start()
+
+    def norm_back(lo, hi):
+        @pl.loop(lo, hi)
+        def _(t):
+            r = tile_rows(t)
+            h = x[r].astype(F32)
+            by_a = da[r].astype(BF).astype(F32)
+            scale = lax.rsqrt(jnp.mean(h * h, -1, keepdims=True) + 1e-6)
+            along = jnp.mean(h * by_a, -1, keepdims=True) * (scale * scale * scale)
+            by_h = (by_a * scale - h * along).astype(BF)
+            x[r] = (dy[r].astype(F32) + by_h.astype(F32)).astype(BF)
+
     s = chunks - 1
     rs_step(s, 0, True)
-    rs_step(s - 1, 2)
-    rs_final(s - 2, last, chunks - 3, True)
-
-    @pl.loop(0, TILES)
-    def _(t):
-        r = tile_rows(t)
-        h = x[r].astype(F32)
-        by_a = da[r].astype(BF).astype(F32)
-        scale = lax.rsqrt(jnp.mean(h * h, -1, keepdims=True) + 1e-6)
-        along = jnp.mean(h * by_a, -1, keepdims=True) * (scale * scale * scale)
-        by_h = (by_a * scale - h * along).astype(BF)
-        x[r] = (dy[r].astype(F32) + by_h.astype(F32)).astype(BF)
-
+    norm_back(0, 2)
+    rs_step(s - 1, 3)
+    norm_back(2, 4)
     rs_step(s, 1)
-    rs_step(s - 1, 3)
     load_a.wait()
 
-    def early(c, point):
-        @pl.when(c == 0)
-        def _():
-            if point == 0:
-                rs_step(s, 2)
-                rs_final(s - 1, last, chunks - 2, True)
-            else:
-                rs_step(s, 3)
-
-        if point == 0:
-
-            @pl.when(c == 1)
-            def _():
-                rs_final(s, last, chunks - 1, True)
-
-    layer_back(0, chunks, x, early)
-
-    s = layers * chunks - 1
-    rs_step(s, 0, True)
-    rs_step(s - 1, 2)
-    rs_final(s - 2, 0, chunks - 3)
-    rs_step(s, 1)
-    rs_step(s - 1, 3)
-    rs_step(s, 2)
-    rs_final(s - 1, 0, chunks - 2)
-    rs_step(s, 3)
-    rs_final(s, 0, chunks - 1)
+    layer_back(
+        0, chunks, x,
+        {
+            (0, 1): lambda: rs_final(s - 1, last, chunks - 2, True),
+            (0, 2): lambda: rs_step(s, 2),
+            (0, 4): lambda: rs_step(s, 3),
+            (1, 1): lambda: rs_final(s, last, chunks - 1, True),
+            (chunks - 1, 4): lambda: rs_step(final_stream, 0, True, parts[0]),
+        },
+    )
+
+    rs_step(final_stream, 0, None, parts[1])
+    rs_step(final_stream - 1, 3)
+    for k in range(1, n // 2):
+        for group in routes_far:
+            for part in parts:
+                rs_step(final_stream, k, None, part, (group,))
+        if k == 1:
+            rs_final(final_stream - 1, 0, chunks - 2)
+    rs_final(final_stream, 0, chunks - 1, None, parts)
 
     others[me] = jnp.full(others.shape[1:], jnp.sum(ss[...]), F32)
     copies = []
@@ -410,12 +443,18 @@
         )
     for copy in copies:
         copy.start()
+    results = [(gg_ref, gg_hbm), (gu_ref, gu_hbm), (gd_ref, gd_hbm)]
+    results = [pltpu.make_async_copy(s, t, local_sem.at[i]) for i, (s, t) in enumerate(results)]
+    for copy in results:
+        copy.start()
     for off in range(1, n):
         slot = others.at[ring(-off)]
         await_bytes(slot, sq_recv.at[off])
     squares_ref[...] = jnp.sum(others[...], axis=0)
     for copy in copies:
         copy.wait_send()
+    for copy in results:
+        copy.wait()
     for u in range(len(units)):
         await_bytes(amount(u), ag_send.at[u])
         await_bytes(amount(u, True), pair_send.at[u])
@@ -450,14 +489,14 @@
         hbm = pl.BlockSpec(memory_space=pl.ANY)
         vmem = pl.BlockSpec(memory_space=pltpu.VMEM)
         dma = pltpu.SemaphoreType.DMA
-        units = [(0, False, 0, 1), (0, False, 1, 2), (0, False, 3, chunks - 3), (0, True, 0, chunks)]
+        units = [(0, False, 0, 1), (0, False, 1, 1), (0, False, 2, chunks - 2), (0, True, 0, chunks)]
         units += [(1, False, 0, chunks), (1, True, 0, chunks)]
         gg, gu, gd, squares, _ = pl.pallas_call(
             functools.partial(step_kernel, n, layers, d_model, ff, tokens, units),
             out_shape=[jax.ShapeDtypeStruct(w.shape, BF) for w in weights]
             + [jax.ShapeDtypeStruct((8, 128), F32), jax.ShapeDtypeStruct((tokens, d_model), BF)],
             in_specs=[hbm] * 5,
-            out_specs=[vmem] * 4 + [hbm],
+            out_specs=[hbm] * 3 + [vmem, hbm],
             scratch_shapes=[
                 pltpu.VMEM((tokens, d_model), BF),
                 pltpu.VMEM((tokens, d_model), BF),
@@ -473,6 +512,7 @@
                 pltpu.VMEM((rows_gu + C // n, C), F32),
                 pltpu.VMEM((n, 8, 128), F32),
                 pltpu.VMEM((2,) + weights[0].shape, BF),
+                *(pltpu.VMEM(w.shape, BF) for w in weights),
                 dma((3,)),
                 dma((2 + layers * chunks,)),
                 dma((len(units), messages)),
@@ -482,6 +522,7 @@
                 dma((len(units),)),
                 dma((len(units),)),
                 dma((3, messages)),
+                dma((2, messages)),
                 dma((3,)),
                 dma((n,)),
                 dma((n,)),

time: 205 us -> 192 us (0.937)
  Pallas kernels: 204 us -> 191 us
    pallas_call x1, Pallas kernels: 199 us -> 186 us  [step(): pl.pallas_call(functools.partial(step_kernel, n, layers, d_model, ff, tok...]
where the time goes in v3:
time: 192 us
  Pallas kernels  191 us (99%)
    pallas_call x1, Pallas kernels, step(): pl.pallas_call(functools.partial(step_kernel, n, layers, d_model, ff, tok...  186 us
    pallas_call x1, Pallas kernels, step(): pl.pallas_call(functools.partial(adamw_kernel, n, float(n * sum((w.size f...  5.74 us

profile of v3, /device:TPU:22, one launch (start us, length us, event | category | flops | bytes accessed | tf_op | source)
XLA Modules:
  0.0 192.2 jit_solution(11169055993021206410)
XLA Ops:
  0.6 185.7 %train_step.1 = (bf16[2,64,1280]{2,1,0:T(8,128)(2,1)}, bf16[2,64,1280]{2,1,0:T(8,128)(2,1)}, bf16[2,160,512]{2,1,0:T(8,128)(2,1)}, f32[8,128]{1,0:T(8,128)}, bf16[4096,512]{1,0:T(8,128)(2,1)}) custom-call(bf16[4096,512]{1,0:T(8,128)(2,1)} %bitcast.2, bf16[4096,512]{1,0:T(8,128)(2,1)} %bitcast.3, bf16[2,64,1280]{2,1,0:T(8,128)(2,1)} %refs_3_.1, ...), custom_call_target="tpu_custom_call" | custom-call | tf_op jit(solution)/shard_map/train_step/pallas_call | solution.py:494
  186.3 5.7 %adamw.1 = (bf16[2,64,1280]{2,1,0:T(8,128)(2,1)}, bf16[2,64,1280]{2,1,0:T(8,128)(2,1)}, bf16[2,160,512]{2,1,0:T(8,128)(2,1)}, f32[2,64,1280]{2,1,0:T(8,128)}, f3...) custom-call(f32[8,128]{1,0:T(8,128)} %get-tuple-element.13.squares, ...), custom_call_target="tpu_custom_call" | custom-call | tf_op jit(solution)/shard_map/adamw/pallas_call | solution.py:537

commit v4 on v3

--- a/solution.py
+++ b/solution.py
@@ -62,9 +62,9 @@
 def step_kernel(
     n, layers, d_model, ff, tokens, units,
     x_hbm, dy_hbm, wg_hbm, wu_hbm, wd_hbm,
-    gg_hbm, gu_hbm, gd_hbm, squares_ref, a_hbm,
-    x, a, dy, da, hidden, wgu, wd, dgu, hid, acc, buf, ss, others, raw, gg_ref, gu_ref, gd_ref,
-    local_sem, own_sem, ag_recv, ag_send, pair_recv, pair_send, side_recv, side_send, rs_recv, rs_last, rs_send, sq_recv, sq_send, credit,
+    gg_hbm, gu_hbm, gd_hbm, squares_ref, a_hbm, both_hbm,
+    x, a, dy, da, hidden, wgu, wd, dgu, hid, acc, buf, ss, others, raw, gg_ref, gu_ref, gd_ref, stage,
+    local_sem, own_sem, ag_recv, ag_send, pair_recv, pair_send, side_recv, side_send, rs_recv, rs_last, rs_send, sq_recv, sq_send, stage_sem, credit,
 ):
     me, rep = lax.axis_index("dp"), lax.axis_index("rep")
     core, row = lax.rem(rep, 2), lax.rem(rep // 2, 2)
@@ -302,7 +302,15 @@
         @pl.loop(lo, lo + 2)
         def _(t):
             r = tile_rows(t)
+            slot = lax.rem(t, 2)
+
+            @pl.when(c * TILES + t >= 2)
+            def _():
+                await_bytes(stage.at[slot], stage_sem.at[slot])
+
             both = dot(a[r], wgu[0, c])
+            stage[slot] = both
+            pltpu.make_async_copy(stage.at[slot], both_hbm.at[c, r], stage_sem.at[slot]).start()
             g, u = both[:, :C], both[:, C:]
             hidden[r, c * C : (c + 1) * C] = (g * sigmoid(g) * u).astype(BF)
 
@@ -316,9 +324,19 @@
         a[r] = normed(h.astype(F32))
     meanwhile[2 * chunks + TILES]()
 
+    for slot in range(2):
+        await_bytes(stage.at[slot], stage_sem.at[slot])
+
+    def fetch(c, t):
+        pltpu.make_async_copy(both_hbm.at[c, tile_rows(t)], stage.at[t % 2], stage_sem.at[t % 2]).start()
+
     def tile_back(l, c, t, back):
         r = tile_rows(t)
-        both = dot(a[r], wgu[l, c])
+        if l == layers - 1:
+            both = dot(a[r], wgu[l, c])
+        else:
+            await_bytes(stage.at[t % 2], stage_sem.at[t % 2])
+            both = stage[t % 2]
         g, u = both[:, :C], both[:, C:]
         dh = dot(back[r], wd[l, c], 1, 1).astype(BF).astype(F32)
         s = sigmoid(g)
@@ -327,6 +345,11 @@
         both = jnp.concatenate([(dh * u * slope).astype(BF), (dh * silu).astype(BF)], axis=1)
         dgu[r] = both
         hid[r] = (silu * u).astype(BF)
+        if l < layers - 1:
+            if t + 2 < TILES:
+                fetch(c, t + 2)
+            else:
+                fetch(lax.rem(c + 1, chunks), t + 2 - TILES)
 
     def add_da(l, c, t):
         if l == layers - 1:
@@ -391,6 +414,8 @@
 
     load_a = pltpu.make_async_copy(a_hbm, a, local_sem.at[2])
     load_a.start()
+    fetch(0, 0)
+    fetch(0, 1)
 
     def norm_back(lo, hi):
         @pl.loop(lo, hi)
@@ -421,6 +446,9 @@
             (chunks - 1, 4): lambda: rs_step(final_stream, 0, True, parts[0]),
         },
     )
+
+    for slot in range(2):
+        await_bytes(stage.at[slot], stage_sem.at[slot])
 
     rs_step(final_stream, 0, None, parts[1])
     rs_step(final_stream - 1, 3)
@@ -443,6 +471,9 @@
         )
     for copy in copies:
         copy.start()
+    for l in range(layers):
+        for ref in (gg_ref, gu_ref):
+            ref[l] = gathered_back(ref[l].astype(F32), n).astype(BF)
     results = [(gg_ref, gg_hbm), (gu_ref, gu_hbm), (gd_ref, gd_hbm)]
     results = [pltpu.make_async_copy(s, t, local_sem.at[i]) for i, (s, t) in enumerate(results)]
     for copy in results:
@@ -462,12 +493,11 @@
             await_bytes(amount(u), side_send.at[u])
 
 
-def adamw_kernel(n, count, squares, *refs):
+def adamw_kernel(count, squares, *refs):
     factor = jnp.minimum(1.0, 0.5 * lax.rsqrt(squares[0:1, 0:1] / count + 1e-30))
     gs, ws, ms, vs, new_w, new_m, new_v = (refs[i : i + 3] for i in range(0, 21, 3))
     for i in range(3):
-        g = gs[i][0].astype(F32) * factor
-        g = (g if i == 2 else gathered_back(g, n))[None]
+        g = gs[i][...].astype(F32) * factor
         m = 0.9 * ms[i][...] + 0.1 * g
         v = 0.95 * vs[i][...] + 0.05 * g * g
         w = ws[i][...].astype(F32)
@@ -491,12 +521,13 @@
         dma = pltpu.SemaphoreType.DMA
         units = [(0, False, 0, 1), (0, False, 1, 1), (0, False, 2, chunks - 2), (0, True, 0, chunks)]
         units += [(1, False, 0, chunks), (1, True, 0, chunks)]
-        gg, gu, gd, squares, _ = pl.pallas_call(
+        gg, gu, gd, squares, *_ = pl.pallas_call(
             functools.partial(step_kernel, n, layers, d_model, ff, tokens, units),
             out_shape=[jax.ShapeDtypeStruct(w.shape, BF) for w in weights]
-            + [jax.ShapeDtypeStruct((8, 128), F32), jax.ShapeDtypeStruct((tokens, d_model), BF)],
+            + [jax.ShapeDtypeStruct((8, 128), F32), jax.ShapeDtypeStruct((tokens, d_model), BF)]
+            + [jax.ShapeDtypeStruct((chunks, tokens, 2 * C), F32)],
             in_specs=[hbm] * 5,
-            out_specs=[hbm] * 3 + [vmem, hbm],
+            out_specs=[hbm] * 3 + [vmem, hbm, hbm],
             scratch_shapes=[
                 pltpu.VMEM((tokens, d_model), BF),
                 pltpu.VMEM((tokens, d_model), BF),
@@ -513,6 +544,7 @@
                 pltpu.VMEM((n, 8, 128), F32),
                 pltpu.VMEM((2,) + weights[0].shape, BF),
                 *(pltpu.VMEM(w.shape, BF) for w in weights),
+                pltpu.VMEM((2, tokens // TILES, 2 * C), F32),
                 dma((3,)),
                 dma((2 + layers * chunks,)),
                 dma((len(units), messages)),
@@ -526,6 +558,7 @@
                 dma((3,)),
                 dma((n,)),
                 dma((n,)),
+                dma((2,)),
                 pltpu.SemaphoreType.REGULAR((2,)),
             ],
             compiler_params=pltpu.CompilerParams(collective_id=0, has_side_effects=True, vmem_limit_bytes=67043328),
@@ -535,7 +568,7 @@
         cut = 2
         specs = [pl.BlockSpec((1, w.shape[1] // cut, w.shape[2]), lambda l, i: (l, i, 0)) for w in weights]
         out = pl.pallas_call(
-            functools.partial(adamw_kernel, n, float(n * sum(w.size for w in weights))),
+            functools.partial(adamw_kernel, float(n * sum(w.size for w in weights))),
             grid=(layers, cut),
             out_shape=[jax.ShapeDtypeStruct(w.shape, dtype) for dtype in (BF, F32, F32) for w in weights],
             in_specs=[pl.BlockSpec((8, 128), lambda l, i: (0, 0))] + specs * 4,

time: 192 us -> 194 us (1.010)
  no operation moved by 1% of the time
where the time goes in v4:
time: 194 us; the launch traced here: 193 us
  Pallas kernels  192 us (99%)
    pallas_call x1, Pallas kernels, step(): pl.pallas_call(functools.partial(step_kernel, n, layers, d_model, ff, tok...  187 us
    pallas_call x1, Pallas kernels, step(): pl.pallas_call(functools.partial(adamw_kernel, float(n * sum((w.size for...  5.58 us

profile of v4, /device:TPU:22, one launch (start us, length us, event | category | flops | bytes accessed | tf_op | source)
XLA Modules:
  0.0 193.3 jit_solution(6171654758047211239)
XLA Ops:
  0.6 186.9 %train_step.1 = (bf16[2,64,1280]{2,1,0:T(8,128)(2,1)}, bf16[2,64,1280]{2,1,0:T(8,128)(2,1)}, bf16[2,160,512]{2,1,0:T(8,128)(2,1)}, f32[8,128]{1,0:T(8,128)}, bf1...) custom-call(bf16[4096,512]{1,0:T(8,128)(2,1)} %bitcast.2, bf16[4096,512]{1,0:T(8,128)(2,1)} %bitcast.3, ...), custom_call_target="tpu_custom_call" | custom-call | tf_op jit(solution)/shard_map/train_step/pallas_call | solution.py:524
  187.5 5.6 %adamw.1 = (bf16[2,64,1280]{2,1,0:T(8,128)(2,1)}, bf16[2,64,1280]{2,1,0:T(8,128)(2,1)}, bf16[2,160,512]{2,1,0:T(8,128)(2,1)}, f32[2,64,1280]{2,1,0:T(8,128)}, f3...) custom-call(f32[8,128]{1,0:T(8,128)} %get-tuple-element.13.squares, ...), custom_call_target="tpu_custom_call" | custom-call | tf_op jit(solution)/shard_map/adamw/pallas_call | solution.py:570
